TPU v7x, 32 devices: a whole 2x2x4 slice. The times are simulated.
32 devices in a mesh: dom: 32 (over z, y, x, core).
Axes of the slice: x: 2, y: 2, z: 4, core: 2. Of those that a mesh axis runs over, the one named last changes fastest.
Arguments:
- start_point: float32 [16384, 128], P('dom'), may hold values from -6 to 6
- residual: float32 [16384, 128], P('dom'), may hold values from -40 to 40
- direction: float32 [16384, 128], P('dom'), may hold values from -40 to 40
- send_list: int32 [32, 4, 3], P('dom'), may hold values from 0 to 3, as said below
- block_cols: int32 [128, 6], P('dom'), may hold values from 0 to 15, as said below
- block_vals: float32 [128, 6, 128, 128], P('dom'), may hold values from -0.2 to 8.1, as said below
Outputs:
- new_point: float32 [16384, 128], P('dom')
- new_residual: float32 [16384, 128], P('dom')
- new_direction: float32 [16384, 128], P('dom')
Inputs may be any that keep to these rules, and one draw needn't show every extreme that they name: send_list[t, m] lists, in its first entries, the distinct blocks of partition t that the partition at offset -off (off as in the first step) reads; between 1 and 3 of them are read for each pair, and some pair reads 3; the other entries are valid block numbers that are never read. `block_cols`: entry 0 of a block row names the row's own block; a block that couples two partitions appears in both partitions' rows, transposed; the assembled matrix is symmetric positive definite. `block_vals`: stored blocks that no coupling uses are zero.
All inputs are finite; a program needn't handle non-finite values.
Results may differ from a plain program's by a relative error of at most 0.0003.
Values sent between devices are 32-bit elements; how exact they have to be, the bound alone decides.
No kernel may reach another device: no remote copies, remote signals or barrier semaphores. Data moves between devices by JAX's collectives and lax.ppermute only.
A program may use at most 128 MiB of HBM per device.

v0:
```python
import jax
import jax.numpy as jnp
from jax import lax
from jax.sharding import PartitionSpec as P

STEPS = 6
BASIS = 13
center_value = 4.5
half_range = 4.5


def from_behind(shard, axis, by):
    peers = lax.axis_size(axis)
    return lax.ppermute(shard, axis, [(i, (i + by) % peers) for i in range(peers)])


def apply_blocks(blocked, send_rows, block_cols, block_vals):
    block_count, block_rows, width = blocked.shape
    highest = lax.Precision.HIGHEST
    flat_rows = blocked.reshape(block_count, block_rows * width)
    hop_count = send_rows.shape[0] // 2
    own_ids = jnp.arange(block_count, dtype=jnp.int32)
    pieces = [flat_rows]
    for slot_index in range(2 * hop_count):
        offset = slot_index + 1 if slot_index < hop_count else hop_count - 1 - slot_index
        chooser = (send_rows[slot_index][:, None] == own_ids[None, :]).astype(jnp.float32)
        outgoing = jnp.dot(chooser, flat_rows, precision=highest)
        pieces.append(from_behind(outgoing, "dom", -offset))
    ghost_table = jnp.concatenate(pieces, axis=0)
    ghost_ids = jnp.arange(ghost_table.shape[0], dtype=jnp.int32)
    running = jnp.zeros((block_count, block_rows, width), jnp.float32)
    for slot_index in range(block_cols.shape[1]):
        chooser = (block_cols[:, slot_index][:, None] == ghost_ids[None, :]).astype(jnp.float32)
        picked = jnp.dot(chooser, ghost_table, precision=highest).reshape(
            block_count, block_rows, width
        )
        running = running + jnp.einsum(
            "icb,ibw->icw", block_vals[:, slot_index], picked, precision=highest
        )
    return running


def next_vector(vector, send_rows, block_cols, block_vals):
    block_count = block_vals.shape[0]
    block_rows = block_vals.shape[2]
    blocked = vector.reshape(block_count, block_rows, vector.shape[1])
    image_part = apply_blocks(blocked, send_rows, block_cols, block_vals).reshape(vector.shape)
    return (image_part - center_value * vector) / half_range


def basis_change():
    positions = jnp.arange(BASIS)
    row_ids = positions[:, None]
    col_ids = positions[None, :]
    active = (col_ids < STEPS) | (col_ids > STEPS) & (col_ids < BASIS - 1)
    change_table = jnp.where(active & (row_ids == col_ids), center_value, 0.0)
    change_table = change_table + jnp.where(active & (row_ids == col_ids + 1), half_range, 0.0)
    return change_table.astype(jnp.float32)


def coefficient_steps(gram_matrix):
    change_table = basis_change()
    column_count = gram_matrix.shape[0]
    positions = jnp.arange(BASIS)
    point_c = jnp.zeros((column_count, BASIS), jnp.float32)
    resid_c = jnp.broadcast_to((positions == STEPS + 1).astype(jnp.float32), (column_count, BASIS))
    direc_c = jnp.broadcast_to((positions == 0).astype(jnp.float32), (column_count, BASIS))
    highest = lax.Precision.HIGHEST
    for step_index in range(STEPS):
        current = jnp.sum(
            resid_c * jnp.einsum("nab,nb->na", gram_matrix, resid_c, precision=highest), axis=1
        )
        moved_dir = jnp.einsum("ab,nb->na", change_table, direc_c, precision=highest)
        curvature = jnp.sum(
            direc_c * jnp.einsum("nab,nb->na", gram_matrix, moved_dir, precision=highest), axis=1
        )
        alpha_step = current / curvature
        point_c = point_c + alpha_step[:, None] * direc_c
        resid_c = resid_c - alpha_step[:, None] * moved_dir
        following = jnp.sum(
            resid_c * jnp.einsum("nab,nb->na", gram_matrix, resid_c, precision=highest), axis=1
        )
        direc_c = resid_c + (following / current)[:, None] * direc_c
    return (point_c, resid_c, direc_c)


def shards(start_point, residual, direction, send_list, block_cols, block_vals):
    send_rows = send_list[0]
    p_basis = [direction]
    r_basis = [residual]
    for power_step in range(STEPS):
        p_basis.append(next_vector(p_basis[-1], send_rows, block_cols, block_vals))
    for power_step in range(STEPS - 1):
        r_basis.append(next_vector(r_basis[-1], send_rows, block_cols, block_vals))
    basis_stack = jnp.stack(p_basis + r_basis)
    local_gram = jnp.einsum(
        "arn,brn->nab", basis_stack, basis_stack, precision=lax.Precision.HIGHEST
    )
    gram_matrix = lax.psum(local_gram, "dom")
    point_c, resid_c, direc_c = coefficient_steps(gram_matrix)
    highest = lax.Precision.HIGHEST
    new_point = start_point + jnp.einsum("na,arn->rn", point_c, basis_stack, precision=highest)
    new_residual = jnp.einsum("na,arn->rn", resid_c, basis_stack, precision=highest)
    new_direction = jnp.einsum("na,arn->rn", direc_c, basis_stack, precision=highest)
    return (new_point, new_residual, new_direction)


def solution(mesh):
    return jax.shard_map(
        shards,
        mesh=mesh,
        in_specs=(
            P("dom", None),
            P("dom", None),
            P("dom", None),
            P("dom", None, None),
            P("dom", None),
            P("dom", None, None, None),
        ),
        out_specs=(P("dom", None), P("dom", None), P("dom", None)),
        check_vma=False,
    )
```

profile of v0, /device:TPU:0, one launch (start us, length us, event | category | flops | bytes accessed | tf_op | source)
XLA Modules:
  0.0 516.2 jit_solution(13102410080200635533)
XLA Ops:
  7.2 1.2 slice_reduce_fusion.6
  9.9 6.5 %collective-permute-start.24 = (f32[3,16384]{1,0:T(4,128)S(1)}, f32[3,16384]{1,0:T(4,128)S(1)}, u32[]{:S(2)}, u32[]{:S(2)}) collective-permute-start(f32[3,16384]{1,0:T(4,128)S(1)} %fusion.361), channel_id=1, source_target_pairs={{0,31},{1,0},{2,1},{3,2},{4,3},{5,4},{6,5},{7,6},{8,7},{9,8},{10,9... | collective-permute-start | bytes 589832 | tf_op jit(solution)/shard_map/ppermute | solution.py:14
  18.6 1.3 collective-permute-start.27
  21.1 5.0 collective-permute-start
  32.6 7.7 %collective-permute-start.3 = (f32[3,16384]{1,0:T(4,128)}, f32[3,16384]{1,0:T(4,128)}, u32[]{:S(2)}, u32[]{:S(2)}) collective-permute-start(f32[3,16384]{1,0:T(4,128)} %fusion.334), channel_id=1, source_target_pairs={{0,2},{1,3},{2,4},{3,5},{4,6},{5,7},{6,8},{7,9},{8,10},{9,11},{10,... | collective-permute-start | bytes 589832 | tf_op jit(solution)/shard_map/ppermute | solution.py:14
  40.3 2.2 concatenate.39
  48.8 1.1 fusion.360
  53.3 6.4 %concatenate.33 = f32[16,16384]{1,0:T(8,128)S(1)} concatenate(f32[4,16384]{1,0:T(4,128)S(1)} %reshape_reshape.33, f32[3,16384]{1,0:T(4,128)} %collective-permute-done, f32[3,16384]{1,0:T(4,128)} %collective-permute-done.1, f32[3,16384]{1,0:T(4,128)} %collective-permute-done.2, f32[3,16384]{1,0:T(4,128)} %collective-permute-done.3), dimensions={0} | concatenate | bytes 2097152 | tf_op jit(solution)/shard_map/concatenate | solution.py:29
  69.0 2.6 collective-permute-start.28
  71.7 1.9 collective-permute-start.31
  73.6 5.0 collective-permute-start.4
  80.6 1.1 fusion.333
  81.7 1.9 collective-permute-start.5
  83.7 12.6 %collective-permute-start.7 = (f32[3,16384]{1,0:T(4,128)}, f32[3,16384]{1,0:T(4,128)}, u32[]{:S(2)}, u32[]{:S(2)}) collective-permute-start(f32[3,16384]{1,0:T(4,128)} %fusion.333), channel_id=1, source_target_pairs={{0,2},{1,3},{2,4},{3,5},{4,6},{5,7},{6,8},{7,9},{8,10},{9,11},{10,... | collective-permute-start | bytes 589832 | tf_op jit(solution)/shard_map/ppermute | solution.py:14
  96.2 6.5 %concatenate.40 = f32[16,16384]{1,0:T(8,128)S(1)} concatenate(f32[4,16384]{1,0:T(4,128)S(1)} %reshape_reshape.40, f32[3,16384]{1,0:T(4,128)} %copy-done.37, f32[3,16384]{1,0:T(4,128)} %copy-done.40, f32[3,16384]{1,0:T(4,128)} %copy-done.43, f32[3,16384]{1,0:T(4,128)} %collective-permute-done.31), dimensions={0} | concatenate | bytes 2097152 | tf_op jit(solution)/shard_map/concatenate | solution.py:29
  109.3 1.1 fusion.348
  113.2 6.7 %concatenate.34 = f32[16,16384]{1,0:T(8,128)S(1)} concatenate(f32[4,16384]{1,0:T(4,128)S(1)} %reshape_reshape.34, f32[3,16384]{1,0:T(4,128)} %collective-permute-done.4, f32[3,16384]{1,0:T(4,128)} %collective-permute-done.5, f32[3,16384]{1,0:T(4,128)} %collective-permute-done.6, f32[3,16384]{1,0:T(4,128)} %collective-permute-done.7), dimensions={0} | concatenate | bytes 2097152 | tf_op jit(solution)/shard_map/concatenate | solution.py:29
  126.4 1.1 fusion.343
  130.8 1.7 collective-permute-start.34
  132.9 4.6 collective-permute-start.32
  137.5 1.2 fusion.365
  139.3 1.5 collective-permute-done.34
  140.8 10.1 %collective-permute-start.9 = (f32[3,16384]{1,0:T(4,128)}, f32[3,16384]{1,0:T(4,128)}, u32[]{:S(2)}, u32[]{:S(2)}) collective-permute-start(f32[3,16384]{1,0:T(4,128)} %fusion.354), channel_id=1, source_target_pairs={{0,30},{1,31},{2,0},{3,1},{4,2},{5,3},{6,4},{7,5},{8,6},{9,7},{10,... | collective-permute-start | bytes 589832 | tf_op jit(solution)/shard_map/ppermute | solution.py:14
  151.0 5.4 %collective-permute-start.8 = (f32[3,16384]{1,0:T(4,128)}, f32[3,16384]{1,0:T(4,128)}, u32[]{:S(2)}, u32[]{:S(2)}) collective-permute-start(f32[3,16384]{1,0:T(4,128)} %fusion.365), channel_id=1, source_target_pairs={{0,31},{1,0},{2,1},{3,2},{4,3},{5,4},{6,5},{7,6},{8,7},{9,8},{10,9... | collective-permute-start | bytes 589832 | tf_op jit(solution)/shard_map/ppermute | solution.py:14
  156.4 3.3 concatenate.41
  166.3 1.1 fusion.358
  170.9 6.4 %concatenate.35 = f32[16,16384]{1,0:T(8,128)S(1)} concatenate(f32[4,16384]{1,0:T(4,128)S(1)} %reshape_reshape.35, f32[3,16384]{1,0:T(4,128)} %collective-permute-done.8, f32[3,16384]{1,0:T(4,128)} %collective-permute-done.9, f32[3,16384]{1,0:T(4,128)} %collective-permute-done.10, f32[3,16384]{1,0:T(4,128)} %collective-permute-done.11), dimensions={0} | concatenate | bytes 2097152 | tf_op jit(solution)/shard_map/concatenate | solution.py:29
  183.9 1.1 fusion.364
  188.2 3.5 collective-permute-start.38
  191.7 2.6 collective-permute-start.39
  195.3 4.1 collective-permute-start.12
  200.4 1.1 fusion.331
  201.6 4.5 collective-permute-done.37
  206.1 6.6 %collective-permute-start.15 = (f32[3,16384]{1,0:T(4,128)}, f32[3,16384]{1,0:T(4,128)}, u32[]{:S(2)}, u32[]{:S(2)}) collective-permute-start(f32[3,16384]{1,0:T(4,128)} %fusion.331), channel_id=1, source_target_pairs={{0,2},{1,3},{2,4},{3,5},{4,6},{5,7},{6,8},{7,9},{8,10},{9,11},{10,... | collective-permute-start | bytes 589832 | tf_op jit(solution)/shard_map/ppermute | solution.py:14
  212.7 6.5 %concatenate.42 = f32[16,16384]{1,0:T(8,128)S(1)} concatenate(f32[4,16384]{1,0:T(4,128)S(1)} %reshape_reshape.42, f32[3,16384]{1,0:T(4,128)} %copy-done.38, f32[3,16384]{1,0:T(4,128)} %copy-done.41, f32[3,16384]{1,0:T(4,128)} %copy-done.44, f32[3,16384]{1,0:T(4,128)} %collective-permute-done.39), dimensions={0} | concatenate | bytes 2097152 | tf_op jit(solution)/shard_map/concatenate | solution.py:29
  228.0 1.1 fusion.335
  229.1 1.1 fusion.324
  230.3 6.7 %concatenate.36 = f32[16,16384]{1,0:T(8,128)S(1)} concatenate(f32[4,16384]{1,0:T(4,128)S(1)} %reshape_reshape.36, f32[3,16384]{1,0:T(4,128)} %collective-permute-done.12, f32[3,16384]{1,0:T(4,128)} %collective-permute-done.13, f32[3,16384]{1,0:T(4,128)} %collective-permute-done.14, f32[3,16384]{1,0:T(4,128)} %collective-permute-done.15), dimensions={0} | concatenate | bytes 2097152 | tf_op jit(solution)/shard_map/concatenate | solution.py:29
  245.0 1.2 fusion.341
  246.2 2.7 collective-permute-start.40
  249.2 1.7 collective-permute-start.43
  251.9 5.1 collective-permute-start.16
  257.9 1.1 fusion.330
  259.1 1.4 collective-permute-start.17
  261.5 14.8 %collective-permute-start.19 = (f32[3,16384]{1,0:T(4,128)}, f32[3,16384]{1,0:T(4,128)}, u32[]{:S(2)}, u32[]{:S(2)}) collective-permute-start(f32[3,16384]{1,0:T(4,128)} %fusion.330), channel_id=1, source_target_pairs={{0,2},{1,3},{2,4},{3,5},{4,6},{5,7},{6,8},{7,9},{8,10},{9,11},{10,... | collective-permute-start | bytes 589832 | tf_op jit(solution)/shard_map/ppermute | solution.py:14
  276.4 6.2 %concatenate.43 = f32[16,16384]{1,0:T(8,128)S(1)} concatenate(f32[4,16384]{1,0:T(4,128)S(1)} %reshape_reshape.43, f32[3,16384]{1,0:T(4,128)} %copy-done.39, f32[3,16384]{1,0:T(4,128)} %copy-done.42, f32[3,16384]{1,0:T(4,128)} %copy-done.45, f32[3,16384]{1,0:T(4,128)} %collective-permute-done.43), dimensions={0} | concatenate | bytes 2097152 | tf_op jit(solution)/shard_map/concatenate | solution.py:29
  282.6 1.2 convolution_bitcast_fusion.5
  283.8 1.2 convolution_bitcast_fusion.4
  285.0 1.2 convolution_bitcast_fusion.3
  286.2 1.2 convolution_bitcast_fusion.2
  287.4 1.2 convolution_bitcast_fusion.1
  288.5 1.2 convolution_bitcast_fusion
  289.8 6.4 %concatenate.37 = f32[16,16384]{1,0:T(8,128)S(1)} concatenate(f32[4,16384]{1,0:T(4,128)S(1)} %reshape_reshape.37, f32[3,16384]{1,0:T(4,128)} %collective-permute-done.16, f32[3,16384]{1,0:T(4,128)} %collective-permute-done.17, f32[3,16384]{1,0:T(4,128)} %collective-permute-done.18, f32[3,16384]{1,0:T(4,128)} %collective-permute-done.19), dimensions={0} | concatenate | bytes 2097152 | tf_op jit(solution)/shard_map/concatenate | solution.py:29
  302.7 1.2 fusion.362
  308.4 2.7 collective-permute-start.20
  311.3 1.8 collective-permute-start.23
  314.7 3.0 collective-permute-done.20
  317.6 5.8 %collective-permute-done.21 = f32[3,16384]{1,0:T(4,128)S(1)} collective-permute-done((f32[3,16384]{1,0:T(4,128)}, f32[3,16384]{1,0:T(4,128)S(1)}, u32[]{:S(2)}, u32[]{:S(2)}) %collective-permute-start.21) | collective-permute-done | bytes 196640 | tf_op jit(solution)/shard_map/ppermute | solution.py:14
  324.8 6.2 %concatenate.38 = f32[16,16384]{1,0:T(8,128)S(1)} concatenate(f32[4,16384]{1,0:T(4,128)S(1)} %reshape_reshape.38, f32[3,16384]{1,0:T(4,128)} %copy-done.47, f32[3,16384]{1,0:T(4,128)} %copy-done.49, f32[3,16384]{1,0:T(4,128)} %copy-done.50, f32[3,16384]{1,0:T(4,128)} %collective-permute-done.23), dimensions={0} | concatenate | bytes 2097152 | tf_op jit(solution)/shard_map/concatenate | solution.py:29
  338.0 9.0 %stack.55 = f32[13,512,128]{1,0,2:T(8,128)} concatenate(f32[1,512,128]{1,0,2:T(1,128)S(1)} %copy-done.27, f32[1,512,128]{1,0,2:T(1,128)S(1)} %copy-done.30, f32[1,512,128]{1,0,2:T(1,128)S(1)} %copy-done.32, f32[1,512,128]{1,0,2:T(1,128)S(1)} %copy-done.34, f32[1,512,128]{1,0,2:T(1,128)S(1)} %copy-done.35, f32[1,512,128]{1,0,2:T(1,128)S(1)} %copy.74, f32[1,512,128]{1,0,2:T(1,128)S(1)} %copy.75, ...), dimensions={0} | concatenate | bytes 6815744 | tf_op jit(solution)/shard_map/stack | solution.py:95
  347.0 10.0 %fusion.499 = f32[128,13,13]{2,1,0:T(8,128)} fusion(f32[13,512,128]{1,0,2:T(8,128)} %stack.55), kind=kOutput, calls=%fused_computation.689 | convolution fusion | flops 132907008 | bytes 3494400 | tf_op jit(solution)/shard_map/arn,brn->nab/dot_general | solution.py:96
  357.2 134.9 %all-reduce.2.cloned.1.call-done = f32[128,13,13]{2,1,0:T(8,128)} async-done(((f32[128,13,13]{2,1,0:T(8,128)}), f32[128,13,13]{2,1,0:T(8,128)}) %all-reduce.2.cloned.1.call-update) | async-done | bytes 86544 | tf_op jit(solution)/shard_map/psum | solution.py:99
  492.1 1.9 multiply_reduce_fusion.14
  502.3 4.3 multiply_reduce_fusion
  (480 shorter events, 124.4 us)
Async XLA Ops:
  7.2 12.7 %copy-start.12 = (f32[512,128]{1,0:T(8,128)S(1)}, f32[512,128]{1,0:T(8,128)}, u32[]{:S(2)}) copy-start(f32[512,128]{1,0:T(8,128)} %param.8) | copy-start | bytes 786436
  7.2 484.9 %all-reduce.2.cloned.1.call-start = ((), (), s32[]{:S(2)}) async-start(), calls=%async_computation | async-start | bytes 2097152 | tf_op jit(solution)/shard_map/psum | solution.py:99
  9.5 16.6 %copy-start.13 = (f32[512,128]{1,0:T(8,128)S(1)}, f32[512,128]{1,0:T(8,128)}, u32[]{:S(2)}) copy-start(f32[512,128]{1,0:T(8,128)} %param.7) | copy-start | bytes 786436
  9.9 22.1 %collective-permute-start.24 = (f32[3,16384]{1,0:T(4,128)S(1)}, f32[3,16384]{1,0:T(4,128)S(1)}, u32[]{:S(2)}, u32[]{:S(2)}) collective-permute-start(f32[3,16384]{1,0:T(4,128)S(1)} %fusion.361), channel_id=1, source_target_pairs={{0,31},{1,0},{2,1},{3,2},{4,3},{5,4},{6,5},{7,6},{8,7},{9,8},{10,9... | collective-permute-start | bytes 589832 | tf_op jit(solution)/shard_map/ppermute | solution.py:14
  16.8 15.8 %collective-permute-start.25 = (f32[3,16384]{1,0:T(4,128)S(1)}, f32[3,16384]{1,0:T(4,128)S(1)}, u32[]{:S(2)}, u32[]{:S(2)}) collective-permute-start(f32[3,16384]{1,0:T(4,128)S(1)} %fusion.350), channel_id=1, source_target_pairs={{0,30},{1,31},{2,0},{3,1},{4,2},{5,3},{6,4},{7,5},{8,6},{9,7},{10,... | collective-permute-start | bytes 589832 | tf_op jit(solution)/shard_map/ppermute | solution.py:14
  17.9 14.7 %collective-permute-start.26 = (f32[3,16384]{1,0:T(4,128)S(1)}, f32[3,16384]{1,0:T(4,128)S(1)}, u32[]{:S(2)}, u32[]{:S(2)}) collective-permute-start(f32[3,16384]{1,0:T(4,128)S(1)} %fusion.339), channel_id=1, source_target_pairs={{0,1},{1,2},{2,3},{3,4},{4,5},{5,6},{6,7},{7,8},{8,9},{9,10},{10,1... | collective-permute-start | bytes 589832 | tf_op jit(solution)/shard_map/ppermute | solution.py:14
  18.6 21.8 %collective-permute-start.27 = (f32[3,16384]{1,0:T(4,128)S(1)}, f32[3,16384]{1,0:T(4,128)}, u32[]{:S(2)}, u32[]{:S(2)}) collective-permute-start(f32[3,16384]{1,0:T(4,128)S(1)} %fusion.328), channel_id=1, source_target_pairs={{0,2},{1,3},{2,4},{3,5},{4,6},{5,7},{6,8},{7,9},{8,10},{9,11},{10,... | collective-permute-start | bytes 589832 | tf_op jit(solution)/shard_map/ppermute | solution.py:14
  20.0 9.9 %copy-start.57 = (s32[4,6]{1,0:T(4,128)S(1)}, s32[4,6]{1,0:T(4,128)}, u32[]{:S(2)}) copy-start(s32[4,6]{1,0:T(4,128)} %param.10) | copy-start | bytes 292
  21.1 32.2 %collective-permute-start = (f32[3,16384]{1,0:T(4,128)}, f32[3,16384]{1,0:T(4,128)}, u32[]{:S(2)}, u32[]{:S(2)}) collective-permute-start(f32[3,16384]{1,0:T(4,128)} %fusion.367), channel_id=1, source_target_pairs={{0,31},{1,0},{2,1},{3,2},{4,3},{5,4},{6,5},{7,6},{8,7},{9,8},{10,9... | collective-permute-start | bytes 589832 | tf_op jit(solution)/shard_map/ppermute | solution.py:14
  26.3 22.2 %copy-start.4 = (f32[512,128]{0,1:T(8,128)}, f32[512,128]{0,1:T(8,128)S(1)}, u32[]{:S(2)}) copy-start(f32[512,128]{0,1:T(8,128)S(1)} %copy.60) | copy-start | bytes 786436
  29.8 35.4 %copy-start.2 = (f32[512,128]{0,1:T(8,128)}, f32[512,128]{0,1:T(8,128)S(1)}, u32[]{:S(2)}) copy-start(f32[512,128]{0,1:T(8,128)S(1)} %copy.47) | copy-start | bytes 786436
  32.0 21.3 %collective-permute-start.1 = (f32[3,16384]{1,0:T(4,128)}, f32[3,16384]{1,0:T(4,128)}, u32[]{:S(2)}, u32[]{:S(2)}) collective-permute-start(f32[3,16384]{1,0:T(4,128)} %fusion.356), channel_id=1, source_target_pairs={{0,30},{1,31},{2,0},{3,1},{4,2},{5,3},{6,4},{7,5},{8,6},{9,7},{10,... | collective-permute-start | bytes 589832 | tf_op jit(solution)/shard_map/ppermute | solution.py:14
  32.6 20.7 %collective-permute-start.2 = (f32[3,16384]{1,0:T(4,128)}, f32[3,16384]{1,0:T(4,128)}, u32[]{:S(2)}, u32[]{:S(2)}) collective-permute-start(f32[3,16384]{1,0:T(4,128)} %fusion.345), channel_id=1, source_target_pairs={{0,1},{1,2},{2,3},{3,4},{4,5},{5,6},{6,7},{7,8},{8,9},{9,10},{10,1... | collective-permute-start | bytes 589832 | tf_op jit(solution)/shard_map/ppermute | solution.py:14
  32.6 20.7 %collective-permute-start.3 = (f32[3,16384]{1,0:T(4,128)}, f32[3,16384]{1,0:T(4,128)}, u32[]{:S(2)}, u32[]{:S(2)}) collective-permute-start(f32[3,16384]{1,0:T(4,128)} %fusion.334), channel_id=1, source_target_pairs={{0,2},{1,3},{2,4},{3,5},{4,6},{5,7},{6,8},{7,9},{8,10},{9,11},{10,... | collective-permute-start | bytes 589832 | tf_op jit(solution)/shard_map/ppermute | solution.py:14
  65.2 6.5 %copy-start.51 = (f32[3,16384]{1,0:T(4,128)S(1)}, f32[3,16384]{1,0:T(4,128)}, u32[]{:S(2)}) copy-start(f32[3,16384]{1,0:T(4,128)} %fusion.327) | copy-start | bytes 589828
  65.3 13.4 %copy-start.11 = (f32[512,128]{0,1:T(8,128)S(1)}, f32[512,128]{0,1:T(8,128)}, u32[]{:S(2)}) copy-start(f32[512,128]{0,1:T(8,128)} %copy-done.10) | copy-start | bytes 786436
  69.0 12.8 %collective-permute-start.28 = (f32[3,16384]{1,0:T(4,128)S(1)}, f32[3,16384]{1,0:T(4,128)S(1)}, u32[]{:S(2)}, u32[]{:S(2)}) collective-permute-start(f32[3,16384]{1,0:T(4,128)S(1)} %copy-done.56), channel_id=1, source_target_pairs={{0,31},{1,0},{2,1},{3,2},{4,3},{5,4},{6,5},{7,6},{8,7},{9,8},{10,9... | collective-permute-start | bytes 589832 | tf_op jit(solution)/shard_map/ppermute | solution.py:14
  71.5 12.1 %collective-permute-start.29 = (f32[3,16384]{1,0:T(4,128)S(1)}, f32[3,16384]{1,0:T(4,128)S(1)}, u32[]{:S(2)}, u32[]{:S(2)}) collective-permute-start(f32[3,16384]{1,0:T(4,128)S(1)} %copy-done.55), channel_id=1, source_target_pairs={{0,30},{1,31},{2,0},{3,1},{4,2},{5,3},{6,4},{7,5},{8,6},{9,7},{10,... | collective-permute-start | bytes 589832 | tf_op jit(solution)/shard_map/ppermute | solution.py:14
  71.6 12.1 %collective-permute-start.30 = (f32[3,16384]{1,0:T(4,128)S(1)}, f32[3,16384]{1,0:T(4,128)S(1)}, u32[]{:S(2)}, u32[]{:S(2)}) collective-permute-start(f32[3,16384]{1,0:T(4,128)S(1)} %copy-done.53), channel_id=1, source_target_pairs={{0,1},{1,2},{2,3},{3,4},{4,5},{5,6},{6,7},{7,8},{8,9},{9,10},{10,1... | collective-permute-start | bytes 589832 | tf_op jit(solution)/shard_map/ppermute | solution.py:14
  71.7 24.5 %collective-permute-start.31 = (f32[3,16384]{1,0:T(4,128)S(1)}, f32[3,16384]{1,0:T(4,128)}, u32[]{:S(2)}, u32[]{:S(2)}) collective-permute-start(f32[3,16384]{1,0:T(4,128)S(1)} %copy-done.51), channel_id=1, source_target_pairs={{0,2},{1,3},{2,4},{3,5},{4,6},{5,7},{6,8},{7,9},{8,10},{9,11},{10,... | collective-permute-start | bytes 589832 | tf_op jit(solution)/shard_map/ppermute | solution.py:14
  73.6 39.5 %collective-permute-start.4 = (f32[3,16384]{1,0:T(4,128)}, f32[3,16384]{1,0:T(4,128)}, u32[]{:S(2)}, u32[]{:S(2)}) collective-permute-start(f32[3,16384]{1,0:T(4,128)} %fusion.366), channel_id=1, source_target_pairs={{0,31},{1,0},{2,1},{3,2},{4,3},{5,4},{6,5},{7,6},{8,7},{9,8},{10,9... | collective-permute-start | bytes 589832 | tf_op jit(solution)/shard_map/ppermute | solution.py:14
  81.7 14.5 %copy-start.37 = (f32[3,16384]{1,0:T(4,128)}, f32[3,16384]{1,0:T(4,128)S(1)}, u32[]{:S(2)}) copy-start(f32[3,16384]{1,0:T(4,128)S(1)} %collective-permute-done.28) | copy-start | bytes 589828
  81.7 31.4 %collective-permute-start.5 = (f32[3,16384]{1,0:T(4,128)}, f32[3,16384]{1,0:T(4,128)}, u32[]{:S(2)}, u32[]{:S(2)}) collective-permute-start(f32[3,16384]{1,0:T(4,128)} %fusion.355), channel_id=1, source_target_pairs={{0,30},{1,31},{2,0},{3,1},{4,2},{5,3},{6,4},{7,5},{8,6},{9,7},{10,... | collective-permute-start | bytes 589832 | tf_op jit(solution)/shard_map/ppermute | solution.py:14
  83.6 12.6 %copy-start.40 = (f32[3,16384]{1,0:T(4,128)}, f32[3,16384]{1,0:T(4,128)S(1)}, u32[]{:S(2)}) copy-start(f32[3,16384]{1,0:T(4,128)S(1)} %collective-permute-done.29) | copy-start | bytes 589828
  83.6 29.5 %collective-permute-start.6 = (f32[3,16384]{1,0:T(4,128)}, f32[3,16384]{1,0:T(4,128)}, u32[]{:S(2)}, u32[]{:S(2)}) collective-permute-start(f32[3,16384]{1,0:T(4,128)} %fusion.344), channel_id=1, source_target_pairs={{0,1},{1,2},{2,3},{3,4},{4,5},{5,6},{6,7},{7,8},{8,9},{9,10},{10,1... | collective-permute-start | bytes 589832 | tf_op jit(solution)/shard_map/ppermute | solution.py:14
  83.7 12.6 %copy-start.43 = (f32[3,16384]{1,0:T(4,128)}, f32[3,16384]{1,0:T(4,128)S(1)}, u32[]{:S(2)}) copy-start(f32[3,16384]{1,0:T(4,128)S(1)} %collective-permute-done.30) | copy-start | bytes 589828
  83.7 29.5 %collective-permute-start.7 = (f32[3,16384]{1,0:T(4,128)}, f32[3,16384]{1,0:T(4,128)}, u32[]{:S(2)}, u32[]{:S(2)}) collective-permute-start(f32[3,16384]{1,0:T(4,128)} %fusion.333), channel_id=1, source_target_pairs={{0,2},{1,3},{2,4},{3,5},{4,6},{5,7},{6,8},{7,9},{8,10},{9,11},{10,... | collective-permute-start | bytes 589832 | tf_op jit(solution)/shard_map/ppermute | solution.py:14
  129.8 9.1 %collective-permute-start.33 = (f32[3,16384]{1,0:T(4,128)}, f32[3,16384]{1,0:T(4,128)S(1)}, u32[]{:S(2)}, u32[]{:S(2)}) collective-permute-start(f32[3,16384]{1,0:T(4,128)} %fusion.348), channel_id=1, source_target_pairs={{0,30},{1,31},{2,0},{3,1},{4,2},{5,3},{6,4},{7,5},{8,6},{9,7},{10,... | collective-permute-start | bytes 589832 | tf_op jit(solution)/shard_map/ppermute | solution.py:14
  130.8 10.0 %collective-permute-start.34 = (f32[3,16384]{1,0:T(4,128)S(1)}, f32[3,16384]{1,0:T(4,128)S(1)}, u32[]{:S(2)}, u32[]{:S(2)}) collective-permute-start(f32[3,16384]{1,0:T(4,128)S(1)} %copy-done.54), channel_id=1, source_target_pairs={{0,1},{1,2},{2,3},{3,4},{4,5},{5,6},{6,7},{7,8},{8,9},{9,10},{10,1... | collective-permute-start | bytes 589832 | tf_op jit(solution)/shard_map/ppermute | solution.py:14
  132.5 18.5 %collective-permute-start.35 = (f32[3,16384]{1,0:T(4,128)S(1)}, f32[3,16384]{1,0:T(4,128)S(1)}, u32[]{:S(2)}, u32[]{:S(2)}) collective-permute-start(f32[3,16384]{1,0:T(4,128)S(1)} %copy-done.52), channel_id=1, source_target_pairs={{0,2},{1,3},{2,4},{3,5},{4,6},{5,7},{6,8},{7,9},{8,10},{9,11},{10,... | collective-permute-start | bytes 589832 | tf_op jit(solution)/shard_map/ppermute | solution.py:14
  132.9 23.6 %collective-permute-start.32 = (f32[3,16384]{1,0:T(4,128)S(1)}, f32[3,16384]{1,0:T(4,128)}, u32[]{:S(2)}, u32[]{:S(2)}) collective-permute-start(f32[3,16384]{1,0:T(4,128)S(1)} %fusion.359), channel_id=1, source_target_pairs={{0,31},{1,0},{2,1},{3,2},{4,3},{5,4},{6,5},{7,6},{8,7},{9,8},{10,9... | collective-permute-start | bytes 589832 | tf_op jit(solution)/shard_map/ppermute | solution.py:14
  137.5 33.3 %collective-permute-start.10 = (f32[3,16384]{1,0:T(4,128)}, f32[3,16384]{1,0:T(4,128)}, u32[]{:S(2)}, u32[]{:S(2)}) collective-permute-start(f32[3,16384]{1,0:T(4,128)} %fusion.343), channel_id=1, source_target_pairs={{0,1},{1,2},{2,3},{3,4},{4,5},{5,6},{6,7},{7,8},{8,9},{9,10},{10,1... | collective-permute-start | bytes 589832 | tf_op jit(solution)/shard_map/ppermute | solution.py:14
  138.9 32.0 %collective-permute-start.11 = (f32[3,16384]{1,0:T(4,128)}, f32[3,16384]{1,0:T(4,128)}, u32[]{:S(2)}, u32[]{:S(2)}) collective-permute-start(f32[3,16384]{1,0:T(4,128)} %fusion.332), channel_id=1, source_target_pairs={{0,2},{1,3},{2,4},{3,5},{4,6},{5,7},{6,8},{7,9},{8,10},{9,11},{10,... | collective-permute-start | bytes 589832 | tf_op jit(solution)/shard_map/ppermute | solution.py:14
  140.8 15.6 %copy-start.46 = (f32[3,16384]{1,0:T(4,128)}, f32[3,16384]{1,0:T(4,128)S(1)}, u32[]{:S(2)}) copy-start(f32[3,16384]{1,0:T(4,128)S(1)} %collective-permute-done.34) | copy-start | bytes 589828
  140.8 30.0 %collective-permute-start.9 = (f32[3,16384]{1,0:T(4,128)}, f32[3,16384]{1,0:T(4,128)}, u32[]{:S(2)}, u32[]{:S(2)}) collective-permute-start(f32[3,16384]{1,0:T(4,128)} %fusion.354), channel_id=1, source_target_pairs={{0,30},{1,31},{2,0},{3,1},{4,2},{5,3},{6,4},{7,5},{8,6},{9,7},{10,... | collective-permute-start | bytes 589832 | tf_op jit(solution)/shard_map/ppermute | solution.py:14
  151.0 19.9 %collective-permute-start.8 = (f32[3,16384]{1,0:T(4,128)}, f32[3,16384]{1,0:T(4,128)}, u32[]{:S(2)}, u32[]{:S(2)}) collective-permute-start(f32[3,16384]{1,0:T(4,128)} %fusion.365), channel_id=1, source_target_pairs={{0,31},{1,0},{2,1},{3,2},{4,3},{5,4},{6,5},{7,6},{8,7},{9,8},{10,9... | collective-permute-start | bytes 589832 | tf_op jit(solution)/shard_map/ppermute | solution.py:14
  183.6 10.7 %copy-start.18 = (f32[1,512,128]{1,2,0:T(8,128)S(1)}, f32[1,512,128]{1,2,0:T(8,128)}, u32[]{:S(2)}) copy-start(f32[1,512,128]{1,2,0:T(8,128)} %get-tuple-element.35) | copy-start | bytes 786436
  187.2 14.3 %collective-permute-start.36 = (f32[3,16384]{1,0:T(4,128)}, f32[3,16384]{1,0:T(4,128)S(1)}, u32[]{:S(2)}, u32[]{:S(2)}) collective-permute-start(f32[3,16384]{1,0:T(4,128)} %fusion.358), channel_id=1, source_target_pairs={{0,31},{1,0},{2,1},{3,2},{4,3},{5,4},{6,5},{7,6},{8,7},{9,8},{10,9... | collective-permute-start | bytes 589832 | tf_op jit(solution)/shard_map/ppermute | solution.py:14
  187.9 18.1 %collective-permute-start.37 = (f32[3,16384]{1,0:T(4,128)}, f32[3,16384]{1,0:T(4,128)S(1)}, u32[]{:S(2)}, u32[]{:S(2)}) collective-permute-start(f32[3,16384]{1,0:T(4,128)} %fusion.347), channel_id=1, source_target_pairs={{0,30},{1,31},{2,0},{3,1},{4,2},{5,3},{6,4},{7,5},{8,6},{9,7},{10,... | collective-permute-start | bytes 589832 | tf_op jit(solution)/shard_map/ppermute | solution.py:14
  188.2 17.9 %collective-permute-start.38 = (f32[3,16384]{1,0:T(4,128)}, f32[3,16384]{1,0:T(4,128)S(1)}, u32[]{:S(2)}, u32[]{:S(2)}) collective-permute-start(f32[3,16384]{1,0:T(4,128)} %fusion.336), channel_id=1, source_target_pairs={{0,1},{1,2},{2,3},{3,4},{4,5},{5,6},{6,7},{7,8},{8,9},{9,10},{10,1... | collective-permute-start | bytes 589832 | tf_op jit(solution)/shard_map/ppermute | solution.py:14
  191.7 20.9 %collective-permute-start.39 = (f32[3,16384]{1,0:T(4,128)}, f32[3,16384]{1,0:T(4,128)}, u32[]{:S(2)}, u32[]{:S(2)}) collective-permute-start(f32[3,16384]{1,0:T(4,128)} %fusion.325), channel_id=1, source_target_pairs={{0,2},{1,3},{2,4},{3,5},{4,6},{5,7},{6,8},{7,9},{8,10},{9,11},{10,... | collective-permute-start | bytes 589832 | tf_op jit(solution)/shard_map/ppermute | solution.py:14
  195.3 35.0 %collective-permute-start.12 = (f32[3,16384]{1,0:T(4,128)}, f32[3,16384]{1,0:T(4,128)}, u32[]{:S(2)}, u32[]{:S(2)}) collective-permute-start(f32[3,16384]{1,0:T(4,128)} %fusion.364), channel_id=1, source_target_pairs={{0,31},{1,0},{2,1},{3,2},{4,3},{5,4},{6,5},{7,6},{8,7},{9,8},{10,9... | collective-permute-start | bytes 589832 | tf_op jit(solution)/shard_map/ppermute | solution.py:14
  201.5 11.1 %copy-start.38 = (f32[3,16384]{1,0:T(4,128)}, f32[3,16384]{1,0:T(4,128)S(1)}, u32[]{:S(2)}) copy-start(f32[3,16384]{1,0:T(4,128)S(1)} %collective-permute-done.36) | copy-start | bytes 589828
  201.5 28.7 %collective-permute-start.13 = (f32[3,16384]{1,0:T(4,128)}, f32[3,16384]{1,0:T(4,128)}, u32[]{:S(2)}, u32[]{:S(2)}) collective-permute-start(f32[3,16384]{1,0:T(4,128)} %fusion.353), channel_id=1, source_target_pairs={{0,30},{1,31},{2,0},{3,1},{4,2},{5,3},{6,4},{7,5},{8,6},{9,7},{10,... | collective-permute-start | bytes 589832 | tf_op jit(solution)/shard_map/ppermute | solution.py:14
  206.1 6.6 %copy-start.41 = (f32[3,16384]{1,0:T(4,128)}, f32[3,16384]{1,0:T(4,128)S(1)}, u32[]{:S(2)}) copy-start(f32[3,16384]{1,0:T(4,128)S(1)} %collective-permute-done.37) | copy-start | bytes 589828
  206.1 24.2 %collective-permute-start.14 = (f32[3,16384]{1,0:T(4,128)}, f32[3,16384]{1,0:T(4,128)}, u32[]{:S(2)}, u32[]{:S(2)}) collective-permute-start(f32[3,16384]{1,0:T(4,128)} %fusion.342), channel_id=1, source_target_pairs={{0,1},{1,2},{2,3},{3,4},{4,5},{5,6},{6,7},{7,8},{8,9},{9,10},{10,1... | collective-permute-start | bytes 589832 | tf_op jit(solution)/shard_map/ppermute | solution.py:14
  206.1 6.6 %copy-start.44 = (f32[3,16384]{1,0:T(4,128)}, f32[3,16384]{1,0:T(4,128)S(1)}, u32[]{:S(2)}) copy-start(f32[3,16384]{1,0:T(4,128)S(1)} %collective-permute-done.38) | copy-start | bytes 589828
  206.1 24.2 %collective-permute-start.15 = (f32[3,16384]{1,0:T(4,128)}, f32[3,16384]{1,0:T(4,128)}, u32[]{:S(2)}, u32[]{:S(2)}) collective-permute-start(f32[3,16384]{1,0:T(4,128)} %fusion.331), channel_id=1, source_target_pairs={{0,2},{1,3},{2,4},{3,5},{4,6},{5,7},{6,8},{7,9},{8,10},{9,11},{10,... | collective-permute-start | bytes 589832 | tf_op jit(solution)/shard_map/ppermute | solution.py:14
  242.5 8.4 %copy-start.19 = (f32[1,512,128]{1,2,0:T(8,128)S(1)}, f32[1,512,128]{1,2,0:T(8,128)}, u32[]{:S(2)}) copy-start(f32[1,512,128]{1,2,0:T(8,128)} %get-tuple-element.34) | copy-start | bytes 786436
  246.2 12.9 %collective-permute-start.40 = (f32[3,16384]{1,0:T(4,128)}, f32[3,16384]{1,0:T(4,128)S(1)}, u32[]{:S(2)}, u32[]{:S(2)}) collective-permute-start(f32[3,16384]{1,0:T(4,128)} %fusion.357), channel_id=1, source_target_pairs={{0,31},{1,0},{2,1},{3,2},{4,3},{5,4},{6,5},{7,6},{8,7},{9,8},{10,9... | collective-permute-start | bytes 589832 | tf_op jit(solution)/shard_map/ppermute | solution.py:14
  248.9 12.6 %collective-permute-start.41 = (f32[3,16384]{1,0:T(4,128)}, f32[3,16384]{1,0:T(4,128)S(1)}, u32[]{:S(2)}, u32[]{:S(2)}) collective-permute-start(f32[3,16384]{1,0:T(4,128)} %fusion.346), channel_id=1, source_target_pairs={{0,30},{1,31},{2,0},{3,1},{4,2},{5,3},{6,4},{7,5},{8,6},{9,7},{10,... | collective-permute-start | bytes 589832 | tf_op jit(solution)/shard_map/ppermute | solution.py:14
  248.9 12.6 %collective-permute-start.42 = (f32[3,16384]{1,0:T(4,128)}, f32[3,16384]{1,0:T(4,128)S(1)}, u32[]{:S(2)}, u32[]{:S(2)}) collective-permute-start(f32[3,16384]{1,0:T(4,128)} %fusion.335), channel_id=1, source_target_pairs={{0,1},{1,2},{2,3},{3,4},{4,5},{5,6},{6,7},{7,8},{8,9},{9,10},{10,1... | collective-permute-start | bytes 589832 | tf_op jit(solution)/shard_map/ppermute | solution.py:14
  249.2 27.2 %collective-permute-start.43 = (f32[3,16384]{1,0:T(4,128)}, f32[3,16384]{1,0:T(4,128)}, u32[]{:S(2)}, u32[]{:S(2)}) collective-permute-start(f32[3,16384]{1,0:T(4,128)} %fusion.324), channel_id=1, source_target_pairs={{0,2},{1,3},{2,4},{3,5},{4,6},{5,7},{6,8},{7,9},{8,10},{9,11},{10,... | collective-permute-start | bytes 589832 | tf_op jit(solution)/shard_map/ppermute | solution.py:14
  251.9 37.8 %collective-permute-start.16 = (f32[3,16384]{1,0:T(4,128)}, f32[3,16384]{1,0:T(4,128)}, u32[]{:S(2)}, u32[]{:S(2)}) collective-permute-start(f32[3,16384]{1,0:T(4,128)} %fusion.363), channel_id=1, source_target_pairs={{0,31},{1,0},{2,1},{3,2},{4,3},{5,4},{6,5},{7,6},{8,7},{9,8},{10,9... | collective-permute-start | bytes 589832 | tf_op jit(solution)/shard_map/ppermute | solution.py:14
  259.1 17.3 %copy-start.39 = (f32[3,16384]{1,0:T(4,128)}, f32[3,16384]{1,0:T(4,128)S(1)}, u32[]{:S(2)}) copy-start(f32[3,16384]{1,0:T(4,128)S(1)} %collective-permute-done.40) | copy-start | bytes 589828
  259.1 30.7 %collective-permute-start.17 = (f32[3,16384]{1,0:T(4,128)}, f32[3,16384]{1,0:T(4,128)}, u32[]{:S(2)}, u32[]{:S(2)}) collective-permute-start(f32[3,16384]{1,0:T(4,128)} %fusion.352), channel_id=1, source_target_pairs={{0,30},{1,31},{2,0},{3,1},{4,2},{5,3},{6,4},{7,5},{8,6},{9,7},{10,... | collective-permute-start | bytes 589832 | tf_op jit(solution)/shard_map/ppermute | solution.py:14
  261.5 14.9 %copy-start.42 = (f32[3,16384]{1,0:T(4,128)}, f32[3,16384]{1,0:T(4,128)S(1)}, u32[]{:S(2)}) copy-start(f32[3,16384]{1,0:T(4,128)S(1)} %collective-permute-done.41) | copy-start | bytes 589828
  261.5 28.2 %collective-permute-start.18 = (f32[3,16384]{1,0:T(4,128)}, f32[3,16384]{1,0:T(4,128)}, u32[]{:S(2)}, u32[]{:S(2)}) collective-permute-start(f32[3,16384]{1,0:T(4,128)} %fusion.341), channel_id=1, source_target_pairs={{0,1},{1,2},{2,3},{3,4},{4,5},{5,6},{6,7},{7,8},{8,9},{9,10},{10,1... | collective-permute-start | bytes 589832 | tf_op jit(solution)/shard_map/ppermute | solution.py:14
  261.5 14.9 %copy-start.45 = (f32[3,16384]{1,0:T(4,128)}, f32[3,16384]{1,0:T(4,128)S(1)}, u32[]{:S(2)}) copy-start(f32[3,16384]{1,0:T(4,128)S(1)} %collective-permute-done.42) | copy-start | bytes 589828
  261.5 28.2 %collective-permute-start.19 = (f32[3,16384]{1,0:T(4,128)}, f32[3,16384]{1,0:T(4,128)}, u32[]{:S(2)}, u32[]{:S(2)}) collective-permute-start(f32[3,16384]{1,0:T(4,128)} %fusion.330), channel_id=1, source_target_pairs={{0,2},{1,3},{2,4},{3,5},{4,6},{5,7},{6,8},{7,9},{8,10},{9,11},{10,... | collective-permute-start | bytes 589832 | tf_op jit(solution)/shard_map/ppermute | solution.py:14
  308.4 9.2 %collective-permute-start.20 = (f32[3,16384]{1,0:T(4,128)}, f32[3,16384]{1,0:T(4,128)S(1)}, u32[]{:S(2)}, u32[]{:S(2)}) collective-permute-start(f32[3,16384]{1,0:T(4,128)} %fusion.362), channel_id=1, source_target_pairs={{0,31},{1,0},{2,1},{3,2},{4,3},{5,4},{6,5},{7,6},{8,7},{9,8},{10,9... | collective-permute-start | bytes 589832 | tf_op jit(solution)/shard_map/ppermute | solution.py:14
  311.1 12.3 %collective-permute-start.21 = (f32[3,16384]{1,0:T(4,128)}, f32[3,16384]{1,0:T(4,128)S(1)}, u32[]{:S(2)}, u32[]{:S(2)}) collective-permute-start(f32[3,16384]{1,0:T(4,128)} %fusion.351), channel_id=1, source_target_pairs={{0,30},{1,31},{2,0},{3,1},{4,2},{5,3},{6,4},{7,5},{8,6},{9,7},{10,... | collective-permute-start | bytes 589832 | tf_op jit(solution)/shard_map/ppermute | solution.py:14
  311.1 12.3 %collective-permute-start.22 = (f32[3,16384]{1,0:T(4,128)S(1)}, f32[3,16384]{1,0:T(4,128)S(1)}, u32[]{:S(2)}, u32[]{:S(2)}) collective-permute-start(f32[3,16384]{1,0:T(4,128)S(1)} %fusion.340), channel_id=1, source_target_pairs={{0,1},{1,2},{2,3},{3,4},{4,5},{5,6},{6,7},{7,8},{8,9},{9,10},{10,1... | collective-permute-start | bytes 589832 | tf_op jit(solution)/shard_map/ppermute | solution.py:14
  311.3 13.5 %collective-permute-start.23 = (f32[3,16384]{1,0:T(4,128)S(1)}, f32[3,16384]{1,0:T(4,128)}, u32[]{:S(2)}, u32[]{:S(2)}) collective-permute-start(f32[3,16384]{1,0:T(4,128)S(1)} %fusion.329), channel_id=1, source_target_pairs={{0,2},{1,3},{2,4},{3,5},{4,6},{5,7},{6,8},{7,9},{8,10},{9,11},{10,... | collective-permute-start | bytes 589832 | tf_op jit(solution)/shard_map/ppermute | solution.py:14
  (39 other events, 93.7 us)
Sparse Core Ops, SparseCore 0:
  357.2 134.8 all-reduce.1
where the time goes:
time: 523 us; the launch traced here: 516 us
  waiting for transfers between devices  151 us (29%)
  starting transfers between devices  119 us (23%)
  matrix products  117 us (22%)
  local copies, waits for them, and re-layouts  95.6 us (18%)
  other arithmetic  17 us (3%)
  between operations  16.7 us (3%)
    psum x1, waiting for transfers between devices, shards(): gram_matrix = lax.psum(local_gram, 'dom')  135 us
    ppermute x44, starting transfers between devices, from_behind(): lax.ppermute(shard, axis, [(i, (i + by) % peers) for i in range(peers)])  118 us
    concatenate x11, local copies, waits for them, and re-layouts, apply_blocks(): ghost_table = jnp.concatenate(pieces, axis=0)  63.5 us
    dot_general x44, matrix products, apply_blocks(): outgoing = jnp.dot(chooser, flat_rows, precision=highest)  44.7 us
    dot_general x66, matrix products, apply_blocks(): jnp.dot(chooser, ghost_table, precision=highest)  36.4 us
    dot_general x66, matrix products, apply_blocks(): jnp.einsum('icb,ibw->icw', block_vals[:, slot_index], picked, precision=h...  25.3 us
    another operation x14, local copies, waits for them, and re-layouts, shards(): basis_stack = jnp.stack(p_basis + r_basis)  18.5 us
    ppermute x44, waiting for transfers between devices, from_behind(): lax.ppermute(shard, axis, [(i, (i + by) % peers) for i in range(peers)])  16 us
  transfers between devices with their start and end apart: 45, of which 7 were waited for; matrix products, arithmetic and copies ran while one was open for 18% of the time, Pallas kernels for 0%

commit v1 on v0

--- a/solution.py
+++ b/solution.py
@@ -96,7 +96,11 @@
     local_gram = jnp.einsum(
         "arn,brn->nab", basis_stack, basis_stack, precision=lax.Precision.HIGHEST
     )
-    gram_matrix = lax.psum(local_gram, "dom")
+    gram_matrix = local_gram
+    for hop in (1, 2, 4, 8, 16):
+        gram_matrix = gram_matrix + lax.ppermute(
+            gram_matrix, "dom", [(dev, dev ^ hop) for dev in range(32)]
+        )
     point_c, resid_c, direc_c = coefficient_steps(gram_matrix)
     highest = lax.Precision.HIGHEST
     new_point = start_point + jnp.einsum("na,arn->rn", point_c, basis_stack, precision=highest)

time: 523 us -> 422 us (0.81)
  waiting for transfers between devices: 151 us -> 30.2 us
  local copies, waits for them, and re-layouts: 95.6 us -> 109 us
  between operations: 16.7 us -> 3.4 us
  starting transfers between devices: 119 us -> 130 us
    psum x1 -> x0, waiting for transfers between devices: 135 us -> none  [shards(): gram_matrix = lax.psum(local_gram, 'dom')]
    ppermute x0 -> x5, waiting for transfers between devices: none -> 15.7 us  [shards(): lax.ppermute(gram_matrix, 'dom', [(dev, dev ^ hop) for dev in range(32)])]
    ppermute x0 -> x5, starting transfers between devices: none -> 10.3 us  [shards(): lax.ppermute(gram_matrix, 'dom', [(dev, dev ^ hop) for dev in range(32)])]
    ppermute x0 -> x5, local copies, waits for them, and re-layouts: none -> 7.02 us  [shards(): lax.ppermute(gram_matrix, 'dom', [(dev, dev ^ hop) for dev in range(32)])]
    add x0 -> x4, other arithmetic: none -> 5.43 us  [shards(): gram_matrix + lax.ppermute(gram_matrix, 'dom', [(dev, dev ^ hop) for dev...]
  transfers between devices with their start and end apart: 45 -> 49, of which waited for: 7 -> 12; matrix products, arithmetic and copies ran while one was open for 18% -> 23% of each run, Pallas kernels for 0% -> 0%
where the time goes in v1:
time: 422 us; the launch traced here: 414 us
  starting transfers between devices  130 us (31%)
  matrix products  119 us (28%)
  local copies, waits for them, and re-layouts  109 us (26%)
  waiting for transfers between devices  30.2 us (7%)
  other arithmetic  22 us (5%)
    ppermute x44, starting transfers between devices, from_behind(): lax.ppermute(shard, axis, [(i, (i + by) % peers) for i in range(peers)])  120 us
    concatenate x11, local copies, waits for them, and re-layouts, apply_blocks(): ghost_table = jnp.concatenate(pieces, axis=0)  62.8 us
    dot_general x44, matrix products, apply_blocks(): outgoing = jnp.dot(chooser, flat_rows, precision=highest)  47.6 us
    dot_general x66, matrix products, apply_blocks(): jnp.dot(chooser, ghost_table, precision=highest)  36.4 us
    dot_general x66, matrix products, apply_blocks(): jnp.einsum('icb,ibw->icw', block_vals[:, slot_index], picked, precision=h...  25.2 us
    another operation x14, local copies, waits for them, and re-layouts, shards(): basis_stack = jnp.stack(p_basis + r_basis)  21.9 us
    ppermute x5, waiting for transfers between devices, shards(): lax.ppermute(gram_matrix, 'dom', [(dev, dev ^ hop) for dev in range(32)])  15.7 us
    ppermute x44, waiting for transfers between devices, from_behind(): lax.ppermute(shard, axis, [(i, (i + by) % peers) for i in range(peers)])  14.5 us
  transfers between devices with their start and end apart: 49, of which 12 were waited for; matrix products, arithmetic and copies ran while one was open for 23% of the time, Pallas kernels for 0%

profile of v1, /device:TPU:0, one launch (start us, length us, event | category | flops | bytes accessed | tf_op | source)
XLA Modules:
  0.0 414.2 jit_solution(8450069216115239414)
XLA Ops:
  0.6 1.2 slice_reduce_fusion.6
  4.1 6.4 %collective-permute-start.24 = (f32[3,16384]{1,0:T(4,128)}, f32[3,16384]{1,0:T(4,128)S(1)}, u32[]{:S(2)}, u32[]{:S(2)}) collective-permute-start(f32[3,16384]{1,0:T(4,128)} %fusion.361), channel_id=1, source_target_pairs={{0,31},{1,0},{2,1},{3,2},{4,3},{5,4},{6,5},{7,6},{8,7},{9,8},{10,9... | collective-permute-start | bytes 589832 | tf_op jit(solution)/shard_map/ppermute | solution.py:14
  12.6 1.3 collective-permute-start.27
  15.2 5.1 %collective-permute-start = (f32[3,16384]{1,0:T(4,128)}, f32[3,16384]{1,0:T(4,128)}, u32[]{:S(2)}, u32[]{:S(2)}) collective-permute-start(f32[3,16384]{1,0:T(4,128)} %fusion.367), channel_id=1, source_target_pairs={{0,31},{1,0},{2,1},{3,2},{4,3},{5,4},{6,5},{7,6},{8,7},{9,8},{10,9... | collective-permute-start | bytes 589832 | tf_op jit(solution)/shard_map/ppermute | solution.py:14
  26.4 8.3 %collective-permute-start.3 = (f32[3,16384]{1,0:T(4,128)}, f32[3,16384]{1,0:T(4,128)}, u32[]{:S(2)}, u32[]{:S(2)}) collective-permute-start(f32[3,16384]{1,0:T(4,128)} %fusion.334), channel_id=1, source_target_pairs={{0,2},{1,3},{2,4},{3,5},{4,6},{5,7},{6,8},{7,9},{8,10},{9,11},{10,... | collective-permute-start | bytes 589832 | tf_op jit(solution)/shard_map/ppermute | solution.py:14
  34.7 1.4 concatenate.39
  47.5 6.5 %concatenate.33 = f32[16,16384]{1,0:T(8,128)S(1)} concatenate(f32[4,16384]{1,0:T(4,128)S(1)} %reshape_reshape.33, f32[3,16384]{1,0:T(4,128)} %collective-permute-done, f32[3,16384]{1,0:T(4,128)} %collective-permute-done.1, f32[3,16384]{1,0:T(4,128)} %collective-permute-done.2, f32[3,16384]{1,0:T(4,128)} %collective-permute-done.3), dimensions={0} | concatenate | bytes 2097152 | tf_op jit(solution)/shard_map/concatenate | solution.py:29
  63.8 2.6 collective-permute-start.28
  66.5 1.9 collective-permute-start.31
  68.4 5.1 %collective-permute-start.4 = (f32[3,16384]{1,0:T(4,128)}, f32[3,16384]{1,0:T(4,128)S(1)}, u32[]{:S(2)}, u32[]{:S(2)}) collective-permute-start(f32[3,16384]{1,0:T(4,128)} %fusion.366), channel_id=1, source_target_pairs={{0,31},{1,0},{2,1},{3,2},{4,3},{5,4},{6,5},{7,6},{8,7},{9,8},{10,9... | collective-permute-start | bytes 589832 | tf_op jit(solution)/shard_map/ppermute | solution.py:14
  76.6 1.8 collective-permute-start.5
  78.5 12.7 %collective-permute-start.7 = (f32[3,16384]{1,0:T(4,128)}, f32[3,16384]{1,0:T(4,128)}, u32[]{:S(2)}, u32[]{:S(2)}) collective-permute-start(f32[3,16384]{1,0:T(4,128)} %fusion.333), channel_id=1, source_target_pairs={{0,2},{1,3},{2,4},{3,5},{4,6},{5,7},{6,8},{7,9},{8,10},{9,11},{10,... | collective-permute-start | bytes 589832 | tf_op jit(solution)/shard_map/ppermute | solution.py:14
  91.2 6.5 %concatenate.40 = f32[16,16384]{1,0:T(8,128)S(1)} concatenate(f32[4,16384]{1,0:T(4,128)S(1)} %reshape_reshape.40, f32[3,16384]{1,0:T(4,128)} %copy-done.35, f32[3,16384]{1,0:T(4,128)} %copy-done.38, f32[3,16384]{1,0:T(4,128)} %copy-done.41, f32[3,16384]{1,0:T(4,128)} %collective-permute-done.31), dimensions={0} | concatenate | bytes 2097152 | tf_op jit(solution)/shard_map/concatenate | solution.py:29
  109.5 6.7 %concatenate.34 = f32[16,16384]{1,0:T(8,128)S(1)} concatenate(f32[4,16384]{1,0:T(4,128)S(1)} %reshape_reshape.34, f32[3,16384]{1,0:T(4,128)} %copy-done.34, f32[3,16384]{1,0:T(4,128)} %collective-permute-done.5, f32[3,16384]{1,0:T(4,128)} %collective-permute-done.6, f32[3,16384]{1,0:T(4,128)} %collective-permute-done.7), dimensions={0} | concatenate | bytes 2097152 | tf_op jit(solution)/shard_map/concatenate | solution.py:29
  127.2 1.9 collective-permute-start.34
  129.3 4.8 %collective-permute-start.32 = (f32[3,16384]{1,0:T(4,128)S(1)}, f32[3,16384]{1,0:T(4,128)}, u32[]{:S(2)}, u32[]{:S(2)}) collective-permute-start(f32[3,16384]{1,0:T(4,128)S(1)} %copy-done.49), channel_id=1, source_target_pairs={{0,31},{1,0},{2,1},{3,2},{4,3},{5,4},{6,5},{7,6},{8,7},{9,8},{10,9... | collective-permute-start | bytes 589832 | tf_op jit(solution)/shard_map/ppermute | solution.py:14
  135.8 1.2 collective-permute-done.34
  137.0 10.4 %collective-permute-start.9 = (f32[3,16384]{1,0:T(4,128)}, f32[3,16384]{1,0:T(4,128)}, u32[]{:S(2)}, u32[]{:S(2)}) collective-permute-start(f32[3,16384]{1,0:T(4,128)} %fusion.354), channel_id=1, source_target_pairs={{0,30},{1,31},{2,0},{3,1},{4,2},{5,3},{6,4},{7,5},{8,6},{9,7},{10,... | collective-permute-start | bytes 589832 | tf_op jit(solution)/shard_map/ppermute | solution.py:14
  147.4 5.4 %collective-permute-start.8 = (f32[3,16384]{1,0:T(4,128)}, f32[3,16384]{1,0:T(4,128)}, u32[]{:S(2)}, u32[]{:S(2)}) collective-permute-start(f32[3,16384]{1,0:T(4,128)} %fusion.365), channel_id=1, source_target_pairs={{0,31},{1,0},{2,1},{3,2},{4,3},{5,4},{6,5},{7,6},{8,7},{9,8},{10,9... | collective-permute-start | bytes 589832 | tf_op jit(solution)/shard_map/ppermute | solution.py:14
  152.9 3.3 concatenate.41
  167.3 6.4 %concatenate.35 = f32[16,16384]{1,0:T(8,128)S(1)} concatenate(f32[4,16384]{1,0:T(4,128)S(1)} %reshape_reshape.35, f32[3,16384]{1,0:T(4,128)} %collective-permute-done.8, f32[3,16384]{1,0:T(4,128)} %collective-permute-done.9, f32[3,16384]{1,0:T(4,128)} %collective-permute-done.10, f32[3,16384]{1,0:T(4,128)} %collective-permute-done.11), dimensions={0} | concatenate | bytes 2097152 | tf_op jit(solution)/shard_map/concatenate | solution.py:29
  184.4 5.2 %collective-permute-start.37 = (f32[3,16384]{1,0:T(4,128)}, f32[3,16384]{1,0:T(4,128)S(1)}, u32[]{:S(2)}, u32[]{:S(2)}) collective-permute-start(f32[3,16384]{1,0:T(4,128)} %fusion.347), channel_id=1, source_target_pairs={{0,30},{1,31},{2,0},{3,1},{4,2},{5,3},{6,4},{7,5},{8,6},{9,7},{10,... | collective-permute-start | bytes 589832 | tf_op jit(solution)/shard_map/ppermute | solution.py:14
  189.6 1.2 collective-permute-start.39
  191.7 4.1 collective-permute-start.12
  198.0 1.7 collective-permute-start.13
  199.7 2.8 collective-permute-done.37
  202.5 6.8 %collective-permute-start.15 = (f32[3,16384]{1,0:T(4,128)}, f32[3,16384]{1,0:T(4,128)}, u32[]{:S(2)}, u32[]{:S(2)}) collective-permute-start(f32[3,16384]{1,0:T(4,128)} %fusion.331), channel_id=1, source_target_pairs={{0,2},{1,3},{2,4},{3,5},{4,6},{5,7},{6,8},{7,9},{8,10},{9,11},{10,... | collective-permute-start | bytes 589832 | tf_op jit(solution)/shard_map/ppermute | solution.py:14
  209.3 6.5 %concatenate.42 = f32[16,16384]{1,0:T(8,128)S(1)} concatenate(f32[4,16384]{1,0:T(4,128)S(1)} %reshape_reshape.42, f32[3,16384]{1,0:T(4,128)} %copy-done.36, f32[3,16384]{1,0:T(4,128)} %copy-done.39, f32[3,16384]{1,0:T(4,128)} %copy-done.42, f32[3,16384]{1,0:T(4,128)} %collective-permute-done.39), dimensions={0} | concatenate | bytes 2097152 | tf_op jit(solution)/shard_map/concatenate | solution.py:29
  226.9 6.7 %concatenate.36 = f32[16,16384]{1,0:T(8,128)S(1)} concatenate(f32[4,16384]{1,0:T(4,128)S(1)} %reshape_reshape.36, f32[3,16384]{1,0:T(4,128)} %collective-permute-done.12, f32[3,16384]{1,0:T(4,128)} %collective-permute-done.13, f32[3,16384]{1,0:T(4,128)} %collective-permute-done.14, f32[3,16384]{1,0:T(4,128)} %collective-permute-done.15), dimensions={0} | concatenate | bytes 2097152 | tf_op jit(solution)/shard_map/concatenate | solution.py:29
  242.9 2.7 collective-permute-start.40
  245.7 1.9 collective-permute-start.43
  248.6 5.1 %collective-permute-start.16 = (f32[3,16384]{1,0:T(4,128)}, f32[3,16384]{1,0:T(4,128)}, u32[]{:S(2)}, u32[]{:S(2)}) collective-permute-start(f32[3,16384]{1,0:T(4,128)} %fusion.363), channel_id=1, source_target_pairs={{0,31},{1,0},{2,1},{3,2},{4,3},{5,4},{6,5},{7,6},{8,7},{9,8},{10,9... | collective-permute-start | bytes 589832 | tf_op jit(solution)/shard_map/ppermute | solution.py:14
  255.8 1.2 collective-permute-start.17
  257.0 2.1 collective-permute-done.41
  259.1 13.5 %collective-permute-start.19 = (f32[3,16384]{1,0:T(4,128)}, f32[3,16384]{1,0:T(4,128)}, u32[]{:S(2)}, u32[]{:S(2)}) collective-permute-start(f32[3,16384]{1,0:T(4,128)} %fusion.330), channel_id=1, source_target_pairs={{0,2},{1,3},{2,4},{3,5},{4,6},{5,7},{6,8},{7,9},{8,10},{9,11},{10,... | collective-permute-start | bytes 589832 | tf_op jit(solution)/shard_map/ppermute | solution.py:14
  272.7 6.2 %concatenate.43 = f32[16,16384]{1,0:T(8,128)S(1)} concatenate(f32[4,16384]{1,0:T(4,128)S(1)} %reshape_reshape.43, f32[3,16384]{1,0:T(4,128)} %copy-done.37, f32[3,16384]{1,0:T(4,128)} %copy-done.40, f32[3,16384]{1,0:T(4,128)} %copy-done.43, f32[3,16384]{1,0:T(4,128)} %collective-permute-done.43), dimensions={0} | concatenate | bytes 2097152 | tf_op jit(solution)/shard_map/concatenate | solution.py:29
  278.9 1.2 convolution_bitcast_fusion.5
  286.1 6.4 %concatenate.37 = f32[16,16384]{1,0:T(8,128)S(1)} concatenate(f32[4,16384]{1,0:T(4,128)S(1)} %reshape_reshape.37, f32[3,16384]{1,0:T(4,128)} %collective-permute-done.16, f32[3,16384]{1,0:T(4,128)} %collective-permute-done.17, f32[3,16384]{1,0:T(4,128)} %collective-permute-done.18, f32[3,16384]{1,0:T(4,128)} %collective-permute-done.19), dimensions={0} | concatenate | bytes 2097152 | tf_op jit(solution)/shard_map/concatenate | solution.py:29
  305.4 2.7 collective-permute-start.20
  308.3 1.8 collective-permute-start.23
  312.3 2.3 collective-permute-done.20
  314.6 5.8 %collective-permute-done.21 = f32[3,16384]{1,0:T(4,128)S(1)} collective-permute-done((f32[3,16384]{1,0:T(4,128)}, f32[3,16384]{1,0:T(4,128)S(1)}, u32[]{:S(2)}, u32[]{:S(2)}) %collective-permute-start.21) | collective-permute-done | bytes 196640 | tf_op jit(solution)/shard_map/ppermute | solution.py:14
  321.8 6.2 %concatenate.38 = f32[16,16384]{1,0:T(8,128)S(1)} concatenate(f32[4,16384]{1,0:T(4,128)S(1)} %reshape_reshape.38, f32[3,16384]{1,0:T(4,128)} %copy-done.45, f32[3,16384]{1,0:T(4,128)} %copy-done.47, f32[3,16384]{1,0:T(4,128)} %copy-done.48, f32[3,16384]{1,0:T(4,128)} %collective-permute-done.23), dimensions={0} | concatenate | bytes 2097152 | tf_op jit(solution)/shard_map/concatenate | solution.py:29
  334.9 11.8 %stack.55 = f32[13,512,128]{1,0,2:T(8,128)} concatenate(f32[1,512,128]{1,0,2:T(1,128)S(1)} %copy-done.25, f32[1,512,128]{1,0,2:T(1,128)S(1)} %copy-done.28, f32[1,512,128]{1,0,2:T(1,128)S(1)} %copy-done.30, f32[1,512,128]{1,0,2:T(1,128)S(1)} %copy-done.32, f32[1,512,128]{1,0,2:T(1,128)} %copy.113, f32[1,512,128]{1,0,2:T(1,128)S(1)} %copy.114, f32[1,512,128]{1,0,2:T(1,128)S(1)} %copy.115, ...), dimensions={0} | concatenate | bytes 6815744 | tf_op jit(solution)/shard_map/stack | solution.py:95
  346.7 9.0 %fusion.499 = f32[128,13,13]{2,1,0:T(8,128)S(1)} fusion(f32[13,512,128]{1,0,2:T(8,128)} %stack.55), kind=kOutput, calls=%fused_computation.689 | convolution fusion | flops 132907008 | bytes 3494400 | tf_op jit(solution)/shard_map/arn,brn->nab/dot_general | solution.py:96
  356.1 1.6 collective-permute-start.44
  358.6 1.4 copy.121
  360.0 1.4 add.379
  361.8 2.7 collective-permute-start.45
  364.4 3.5 collective-permute-done.45
  367.9 1.4 copy.123
  369.3 1.4 add.380
  371.1 4.0 collective-permute-start.46
  375.0 2.7 collective-permute-done.46
  377.7 1.4 copy.125
  379.1 1.4 add.381
  381.3 4.4 %collective-permute-done.47 = f32[128,13,13]{0,2,1:T(8,128)S(1)} collective-permute-done((f32[128,13,13]{0,2,1:T(8,128)S(1)}, f32[128,13,13]{0,2,1:T(8,128)S(1)}, u32[]{:S(2)}, u32[]{:S(2)}) %collective-permute-start.47) | collective-permute-done | bytes 86560 | tf_op jit(solution)/shard_map/ppermute | solution.py:101
  385.6 1.4 copy.127
  387.0 1.4 add.382
  388.8 2.1 collective-permute-start.48
  390.8 4.2 %collective-permute-done.48 = f32[128,13,13]{0,2,1:T(8,128)S(1)} collective-permute-done((f32[128,13,13]{0,2,1:T(8,128)S(1)}, f32[128,13,13]{0,2,1:T(8,128)S(1)}, u32[]{:S(2)}, u32[]{:S(2)}) %collective-permute-start.48) | collective-permute-done | bytes 86560 | tf_op jit(solution)/shard_map/ppermute | solution.py:101
  395.0 1.4 copy.129
  396.4 1.9 multiply_reduce_fusion.14
  406.9 4.2 %multiply_reduce_fusion = (f32[128,512]{1,0:T(8,128)S(1)}, f32[128,512]{1,0:T(8,128)S(1)}, f32[128,512]{1,0:T(8,128)S(1)}) fusion(f32[13,512,128]{1,0,2:T(8,128)} %stack.55, f32[128,13]{1,0:T(8,128)S(1)} %copy.255, f32[128,13]{1,0:T(8,128)S(1)} %copy.253, f32[128,13]{1,0:T(8,128)S(1)} %copy.250), kind=kLoop, calls=%fused_computation | loop fusion | flops 4915200 | bytes 4214272
  (491 shorter events, 151.5 us)
Async XLA Ops:
  0.6 13.3 %copy-start.11 = (f32[512,128]{1,0:T(8,128)S(1)}, f32[512,128]{1,0:T(8,128)}, u32[]{:S(2)}) copy-start(f32[512,128]{1,0:T(8,128)} %param.8) | copy-start | bytes 786436
  2.9 17.3 %copy-start.12 = (f32[512,128]{1,0:T(8,128)S(1)}, f32[512,128]{1,0:T(8,128)}, u32[]{:S(2)}) copy-start(f32[512,128]{1,0:T(8,128)} %param.7) | copy-start | bytes 786436
  4.1 21.8 %collective-permute-start.24 = (f32[3,16384]{1,0:T(4,128)}, f32[3,16384]{1,0:T(4,128)S(1)}, u32[]{:S(2)}, u32[]{:S(2)}) collective-permute-start(f32[3,16384]{1,0:T(4,128)} %fusion.361), channel_id=1, source_target_pairs={{0,31},{1,0},{2,1},{3,2},{4,3},{5,4},{6,5},{7,6},{8,7},{9,8},{10,9... | collective-permute-start | bytes 589832 | tf_op jit(solution)/shard_map/ppermute | solution.py:14
  10.9 15.5 %collective-permute-start.25 = (f32[3,16384]{1,0:T(4,128)S(1)}, f32[3,16384]{1,0:T(4,128)S(1)}, u32[]{:S(2)}, u32[]{:S(2)}) collective-permute-start(f32[3,16384]{1,0:T(4,128)S(1)} %fusion.350), channel_id=1, source_target_pairs={{0,30},{1,31},{2,0},{3,1},{4,2},{5,3},{6,4},{7,5},{8,6},{9,7},{10,... | collective-permute-start | bytes 589832 | tf_op jit(solution)/shard_map/ppermute | solution.py:14
  11.9 14.5 %collective-permute-start.26 = (f32[3,16384]{1,0:T(4,128)S(1)}, f32[3,16384]{1,0:T(4,128)S(1)}, u32[]{:S(2)}, u32[]{:S(2)}) collective-permute-start(f32[3,16384]{1,0:T(4,128)S(1)} %fusion.339), channel_id=1, source_target_pairs={{0,1},{1,2},{2,3},{3,4},{4,5},{5,6},{6,7},{7,8},{8,9},{9,10},{10,1... | collective-permute-start | bytes 589832 | tf_op jit(solution)/shard_map/ppermute | solution.py:14
  12.6 10.1 %copy-start.52 = (s32[4,6]{1,0:T(4,128)S(1)}, s32[4,6]{1,0:T(4,128)}, u32[]{:S(2)}) copy-start(s32[4,6]{1,0:T(4,128)} %param.10) | copy-start | bytes 292
  12.6 22.0 %collective-permute-start.27 = (f32[3,16384]{1,0:T(4,128)S(1)}, f32[3,16384]{1,0:T(4,128)S(1)}, u32[]{:S(2)}, u32[]{:S(2)}) collective-permute-start(f32[3,16384]{1,0:T(4,128)S(1)} %fusion.328), channel_id=1, source_target_pairs={{0,2},{1,3},{2,4},{3,5},{4,6},{5,7},{6,8},{7,9},{8,10},{9,11},{10,... | collective-permute-start | bytes 589832 | tf_op jit(solution)/shard_map/ppermute | solution.py:14
  15.2 32.3 %collective-permute-start = (f32[3,16384]{1,0:T(4,128)}, f32[3,16384]{1,0:T(4,128)}, u32[]{:S(2)}, u32[]{:S(2)}) collective-permute-start(f32[3,16384]{1,0:T(4,128)} %fusion.367), channel_id=1, source_target_pairs={{0,31},{1,0},{2,1},{3,2},{4,3},{5,4},{6,5},{7,6},{8,7},{9,8},{10,9... | collective-permute-start | bytes 589832 | tf_op jit(solution)/shard_map/ppermute | solution.py:14
  20.4 21.6 %copy-start.3 = (f32[512,128]{0,1:T(8,128)}, f32[512,128]{0,1:T(8,128)S(1)}, u32[]{:S(2)}) copy-start(f32[512,128]{0,1:T(8,128)S(1)} %copy.100) | copy-start | bytes 786436
  22.8 36.7 %copy-start.1 = (f32[512,128]{0,1:T(8,128)}, f32[512,128]{0,1:T(8,128)S(1)}, u32[]{:S(2)}) copy-start(f32[512,128]{0,1:T(8,128)S(1)} %copy.87) | copy-start | bytes 786436
  25.9 21.7 %collective-permute-start.1 = (f32[3,16384]{1,0:T(4,128)}, f32[3,16384]{1,0:T(4,128)}, u32[]{:S(2)}, u32[]{:S(2)}) collective-permute-start(f32[3,16384]{1,0:T(4,128)} %fusion.356), channel_id=1, source_target_pairs={{0,30},{1,31},{2,0},{3,1},{4,2},{5,3},{6,4},{7,5},{8,6},{9,7},{10,... | collective-permute-start | bytes 589832 | tf_op jit(solution)/shard_map/ppermute | solution.py:14
  26.4 21.1 %collective-permute-start.2 = (f32[3,16384]{1,0:T(4,128)}, f32[3,16384]{1,0:T(4,128)}, u32[]{:S(2)}, u32[]{:S(2)}) collective-permute-start(f32[3,16384]{1,0:T(4,128)} %fusion.345), channel_id=1, source_target_pairs={{0,1},{1,2},{2,3},{3,4},{4,5},{5,6},{6,7},{7,8},{8,9},{9,10},{10,1... | collective-permute-start | bytes 589832 | tf_op jit(solution)/shard_map/ppermute | solution.py:14
  26.4 21.1 %collective-permute-start.3 = (f32[3,16384]{1,0:T(4,128)}, f32[3,16384]{1,0:T(4,128)}, u32[]{:S(2)}, u32[]{:S(2)}) collective-permute-start(f32[3,16384]{1,0:T(4,128)} %fusion.334), channel_id=1, source_target_pairs={{0,2},{1,3},{2,4},{3,5},{4,6},{5,7},{6,8},{7,9},{8,10},{9,11},{10,... | collective-permute-start | bytes 589832 | tf_op jit(solution)/shard_map/ppermute | solution.py:14
  59.5 14.0 %copy-start.10 = (f32[512,128]{0,1:T(8,128)S(1)}, f32[512,128]{0,1:T(8,128)}, u32[]{:S(2)}) copy-start(f32[512,128]{0,1:T(8,128)} %copy-done.9) | copy-start | bytes 786436
  63.8 12.8 %collective-permute-start.28 = (f32[3,16384]{1,0:T(4,128)}, f32[3,16384]{1,0:T(4,128)S(1)}, u32[]{:S(2)}, u32[]{:S(2)}) collective-permute-start(f32[3,16384]{1,0:T(4,128)} %fusion.360), channel_id=1, source_target_pairs={{0,31},{1,0},{2,1},{3,2},{4,3},{5,4},{6,5},{7,6},{8,7},{9,8},{10,9... | collective-permute-start | bytes 589832 | tf_op jit(solution)/shard_map/ppermute | solution.py:14
  66.4 12.1 %collective-permute-start.29 = (f32[3,16384]{1,0:T(4,128)}, f32[3,16384]{1,0:T(4,128)S(1)}, u32[]{:S(2)}, u32[]{:S(2)}) collective-permute-start(f32[3,16384]{1,0:T(4,128)} %fusion.349), channel_id=1, source_target_pairs={{0,30},{1,31},{2,0},{3,1},{4,2},{5,3},{6,4},{7,5},{8,6},{9,7},{10,... | collective-permute-start | bytes 589832 | tf_op jit(solution)/shard_map/ppermute | solution.py:14
  66.4 12.1 %collective-permute-start.30 = (f32[3,16384]{1,0:T(4,128)}, f32[3,16384]{1,0:T(4,128)S(1)}, u32[]{:S(2)}, u32[]{:S(2)}) collective-permute-start(f32[3,16384]{1,0:T(4,128)} %fusion.338), channel_id=1, source_target_pairs={{0,1},{1,2},{2,3},{3,4},{4,5},{5,6},{6,7},{7,8},{8,9},{9,10},{10,1... | collective-permute-start | bytes 589832 | tf_op jit(solution)/shard_map/ppermute | solution.py:14
  66.5 24.7 %collective-permute-start.31 = (f32[3,16384]{1,0:T(4,128)}, f32[3,16384]{1,0:T(4,128)}, u32[]{:S(2)}, u32[]{:S(2)}) collective-permute-start(f32[3,16384]{1,0:T(4,128)} %fusion.327), channel_id=1, source_target_pairs={{0,2},{1,3},{2,4},{3,5},{4,6},{5,7},{6,8},{7,9},{8,10},{9,11},{10,... | collective-permute-start | bytes 589832 | tf_op jit(solution)/shard_map/ppermute | solution.py:14
  68.4 40.4 %collective-permute-start.4 = (f32[3,16384]{1,0:T(4,128)}, f32[3,16384]{1,0:T(4,128)S(1)}, u32[]{:S(2)}, u32[]{:S(2)}) collective-permute-start(f32[3,16384]{1,0:T(4,128)} %fusion.366), channel_id=1, source_target_pairs={{0,31},{1,0},{2,1},{3,2},{4,3},{5,4},{6,5},{7,6},{8,7},{9,8},{10,9... | collective-permute-start | bytes 589832 | tf_op jit(solution)/shard_map/ppermute | solution.py:14
  76.6 14.6 %copy-start.35 = (f32[3,16384]{1,0:T(4,128)}, f32[3,16384]{1,0:T(4,128)S(1)}, u32[]{:S(2)}) copy-start(f32[3,16384]{1,0:T(4,128)S(1)} %collective-permute-done.28) | copy-start | bytes 589828
  76.6 32.3 %collective-permute-start.5 = (f32[3,16384]{1,0:T(4,128)}, f32[3,16384]{1,0:T(4,128)}, u32[]{:S(2)}, u32[]{:S(2)}) collective-permute-start(f32[3,16384]{1,0:T(4,128)} %fusion.355), channel_id=1, source_target_pairs={{0,30},{1,31},{2,0},{3,1},{4,2},{5,3},{6,4},{7,5},{8,6},{9,7},{10,... | collective-permute-start | bytes 589832 | tf_op jit(solution)/shard_map/ppermute | solution.py:14
  78.5 12.7 %copy-start.38 = (f32[3,16384]{1,0:T(4,128)}, f32[3,16384]{1,0:T(4,128)S(1)}, u32[]{:S(2)}) copy-start(f32[3,16384]{1,0:T(4,128)S(1)} %collective-permute-done.29) | copy-start | bytes 589828
  78.5 30.3 %collective-permute-start.6 = (f32[3,16384]{1,0:T(4,128)}, f32[3,16384]{1,0:T(4,128)}, u32[]{:S(2)}, u32[]{:S(2)}) collective-permute-start(f32[3,16384]{1,0:T(4,128)} %fusion.344), channel_id=1, source_target_pairs={{0,1},{1,2},{2,3},{3,4},{4,5},{5,6},{6,7},{7,8},{8,9},{9,10},{10,1... | collective-permute-start | bytes 589832 | tf_op jit(solution)/shard_map/ppermute | solution.py:14
  78.5 12.7 %copy-start.41 = (f32[3,16384]{1,0:T(4,128)}, f32[3,16384]{1,0:T(4,128)S(1)}, u32[]{:S(2)}) copy-start(f32[3,16384]{1,0:T(4,128)S(1)} %collective-permute-done.30) | copy-start | bytes 589828
  78.5 31.0 %collective-permute-start.7 = (f32[3,16384]{1,0:T(4,128)}, f32[3,16384]{1,0:T(4,128)}, u32[]{:S(2)}, u32[]{:S(2)}) collective-permute-start(f32[3,16384]{1,0:T(4,128)} %fusion.333), channel_id=1, source_target_pairs={{0,2},{1,3},{2,4},{3,5},{4,6},{5,7},{6,8},{7,9},{8,10},{9,11},{10,... | collective-permute-start | bytes 589832 | tf_op jit(solution)/shard_map/ppermute | solution.py:14
  126.3 9.1 %collective-permute-start.33 = (f32[3,16384]{1,0:T(4,128)}, f32[3,16384]{1,0:T(4,128)S(1)}, u32[]{:S(2)}, u32[]{:S(2)}) collective-permute-start(f32[3,16384]{1,0:T(4,128)} %fusion.348), channel_id=1, source_target_pairs={{0,30},{1,31},{2,0},{3,1},{4,2},{5,3},{6,4},{7,5},{8,6},{9,7},{10,... | collective-permute-start | bytes 589832 | tf_op jit(solution)/shard_map/ppermute | solution.py:14
  127.2 9.8 %collective-permute-start.34 = (f32[3,16384]{1,0:T(4,128)S(1)}, f32[3,16384]{1,0:T(4,128)S(1)}, u32[]{:S(2)}, u32[]{:S(2)}) collective-permute-start(f32[3,16384]{1,0:T(4,128)S(1)} %copy-done.51), channel_id=1, source_target_pairs={{0,1},{1,2},{2,3},{3,4},{4,5},{5,6},{6,7},{7,8},{8,9},{9,10},{10,1... | collective-permute-start | bytes 589832 | tf_op jit(solution)/shard_map/ppermute | solution.py:14
  129.1 18.4 %collective-permute-start.35 = (f32[3,16384]{1,0:T(4,128)S(1)}, f32[3,16384]{1,0:T(4,128)S(1)}, u32[]{:S(2)}, u32[]{:S(2)}) collective-permute-start(f32[3,16384]{1,0:T(4,128)S(1)} %copy-done.50), channel_id=1, source_target_pairs={{0,2},{1,3},{2,4},{3,5},{4,6},{5,7},{6,8},{7,9},{8,10},{9,11},{10,... | collective-permute-start | bytes 589832 | tf_op jit(solution)/shard_map/ppermute | solution.py:14
  129.3 23.6 %collective-permute-start.32 = (f32[3,16384]{1,0:T(4,128)S(1)}, f32[3,16384]{1,0:T(4,128)}, u32[]{:S(2)}, u32[]{:S(2)}) collective-permute-start(f32[3,16384]{1,0:T(4,128)S(1)} %copy-done.49), channel_id=1, source_target_pairs={{0,31},{1,0},{2,1},{3,2},{4,3},{5,4},{6,5},{7,6},{8,7},{9,8},{10,9... | collective-permute-start | bytes 589832 | tf_op jit(solution)/shard_map/ppermute | solution.py:14
  134.1 33.2 %collective-permute-start.10 = (f32[3,16384]{1,0:T(4,128)}, f32[3,16384]{1,0:T(4,128)}, u32[]{:S(2)}, u32[]{:S(2)}) collective-permute-start(f32[3,16384]{1,0:T(4,128)} %fusion.343), channel_id=1, source_target_pairs={{0,1},{1,2},{2,3},{3,4},{4,5},{5,6},{6,7},{7,8},{8,9},{9,10},{10,1... | collective-permute-start | bytes 589832 | tf_op jit(solution)/shard_map/ppermute | solution.py:14
  135.3 32.0 %collective-permute-start.11 = (f32[3,16384]{1,0:T(4,128)}, f32[3,16384]{1,0:T(4,128)}, u32[]{:S(2)}, u32[]{:S(2)}) collective-permute-start(f32[3,16384]{1,0:T(4,128)} %fusion.332), channel_id=1, source_target_pairs={{0,2},{1,3},{2,4},{3,5},{4,6},{5,7},{6,8},{7,9},{8,10},{9,11},{10,... | collective-permute-start | bytes 589832 | tf_op jit(solution)/shard_map/ppermute | solution.py:14
  137.0 15.8 %copy-start.44 = (f32[3,16384]{1,0:T(4,128)}, f32[3,16384]{1,0:T(4,128)S(1)}, u32[]{:S(2)}) copy-start(f32[3,16384]{1,0:T(4,128)S(1)} %collective-permute-done.34) | copy-start | bytes 589828
  137.0 30.3 %collective-permute-start.9 = (f32[3,16384]{1,0:T(4,128)}, f32[3,16384]{1,0:T(4,128)}, u32[]{:S(2)}, u32[]{:S(2)}) collective-permute-start(f32[3,16384]{1,0:T(4,128)} %fusion.354), channel_id=1, source_target_pairs={{0,30},{1,31},{2,0},{3,1},{4,2},{5,3},{6,4},{7,5},{8,6},{9,7},{10,... | collective-permute-start | bytes 589832 | tf_op jit(solution)/shard_map/ppermute | solution.py:14
  147.4 19.9 %collective-permute-start.8 = (f32[3,16384]{1,0:T(4,128)}, f32[3,16384]{1,0:T(4,128)}, u32[]{:S(2)}, u32[]{:S(2)}) collective-permute-start(f32[3,16384]{1,0:T(4,128)} %fusion.365), channel_id=1, source_target_pairs={{0,31},{1,0},{2,1},{3,2},{4,3},{5,4},{6,5},{7,6},{8,7},{9,8},{10,9... | collective-permute-start | bytes 589832 | tf_op jit(solution)/shard_map/ppermute | solution.py:14
  180.1 10.7 %copy-start.17 = (f32[1,512,128]{1,2,0:T(8,128)S(1)}, f32[1,512,128]{1,2,0:T(8,128)}, u32[]{:S(2)}) copy-start(f32[1,512,128]{1,2,0:T(8,128)} %get-tuple-element.36) | copy-start | bytes 786436
  183.7 14.3 %collective-permute-start.36 = (f32[3,16384]{1,0:T(4,128)}, f32[3,16384]{1,0:T(4,128)S(1)}, u32[]{:S(2)}, u32[]{:S(2)}) collective-permute-start(f32[3,16384]{1,0:T(4,128)} %fusion.358), channel_id=1, source_target_pairs={{0,31},{1,0},{2,1},{3,2},{4,3},{5,4},{6,5},{7,6},{8,7},{9,8},{10,9... | collective-permute-start | bytes 589832 | tf_op jit(solution)/shard_map/ppermute | solution.py:14
  184.4 18.1 %collective-permute-start.37 = (f32[3,16384]{1,0:T(4,128)}, f32[3,16384]{1,0:T(4,128)S(1)}, u32[]{:S(2)}, u32[]{:S(2)}) collective-permute-start(f32[3,16384]{1,0:T(4,128)} %fusion.347), channel_id=1, source_target_pairs={{0,30},{1,31},{2,0},{3,1},{4,2},{5,3},{6,4},{7,5},{8,6},{9,7},{10,... | collective-permute-start | bytes 589832 | tf_op jit(solution)/shard_map/ppermute | solution.py:14
  189.6 13.0 %collective-permute-start.38 = (f32[3,16384]{1,0:T(4,128)}, f32[3,16384]{1,0:T(4,128)S(1)}, u32[]{:S(2)}, u32[]{:S(2)}) collective-permute-start(f32[3,16384]{1,0:T(4,128)} %fusion.336), channel_id=1, source_target_pairs={{0,1},{1,2},{2,3},{3,4},{4,5},{5,6},{6,7},{7,8},{8,9},{9,10},{10,1... | collective-permute-start | bytes 589832 | tf_op jit(solution)/shard_map/ppermute | solution.py:14
  189.6 19.8 %collective-permute-start.39 = (f32[3,16384]{1,0:T(4,128)}, f32[3,16384]{1,0:T(4,128)}, u32[]{:S(2)}, u32[]{:S(2)}) collective-permute-start(f32[3,16384]{1,0:T(4,128)} %fusion.325), channel_id=1, source_target_pairs={{0,2},{1,3},{2,4},{3,5},{4,6},{5,7},{6,8},{7,9},{8,10},{9,11},{10,... | collective-permute-start | bytes 589832 | tf_op jit(solution)/shard_map/ppermute | solution.py:14
  191.7 35.2 %collective-permute-start.12 = (f32[3,16384]{1,0:T(4,128)}, f32[3,16384]{1,0:T(4,128)}, u32[]{:S(2)}, u32[]{:S(2)}) collective-permute-start(f32[3,16384]{1,0:T(4,128)} %fusion.364), channel_id=1, source_target_pairs={{0,31},{1,0},{2,1},{3,2},{4,3},{5,4},{6,5},{7,6},{8,7},{9,8},{10,9... | collective-permute-start | bytes 589832 | tf_op jit(solution)/shard_map/ppermute | solution.py:14
  198.0 11.3 %copy-start.36 = (f32[3,16384]{1,0:T(4,128)}, f32[3,16384]{1,0:T(4,128)S(1)}, u32[]{:S(2)}) copy-start(f32[3,16384]{1,0:T(4,128)S(1)} %collective-permute-done.36) | copy-start | bytes 589828
  198.0 28.9 %collective-permute-start.13 = (f32[3,16384]{1,0:T(4,128)}, f32[3,16384]{1,0:T(4,128)}, u32[]{:S(2)}, u32[]{:S(2)}) collective-permute-start(f32[3,16384]{1,0:T(4,128)} %fusion.353), channel_id=1, source_target_pairs={{0,30},{1,31},{2,0},{3,1},{4,2},{5,3},{6,4},{7,5},{8,6},{9,7},{10,... | collective-permute-start | bytes 589832 | tf_op jit(solution)/shard_map/ppermute | solution.py:14
  202.5 24.4 %collective-permute-start.14 = (f32[3,16384]{1,0:T(4,128)}, f32[3,16384]{1,0:T(4,128)}, u32[]{:S(2)}, u32[]{:S(2)}) collective-permute-start(f32[3,16384]{1,0:T(4,128)} %fusion.342), channel_id=1, source_target_pairs={{0,1},{1,2},{2,3},{3,4},{4,5},{5,6},{6,7},{7,8},{8,9},{9,10},{10,1... | collective-permute-start | bytes 589832 | tf_op jit(solution)/shard_map/ppermute | solution.py:14
  202.5 24.4 %collective-permute-start.15 = (f32[3,16384]{1,0:T(4,128)}, f32[3,16384]{1,0:T(4,128)}, u32[]{:S(2)}, u32[]{:S(2)}) collective-permute-start(f32[3,16384]{1,0:T(4,128)} %fusion.331), channel_id=1, source_target_pairs={{0,2},{1,3},{2,4},{3,5},{4,6},{5,7},{6,8},{7,9},{8,10},{9,11},{10,... | collective-permute-start | bytes 589832 | tf_op jit(solution)/shard_map/ppermute | solution.py:14
  242.9 12.9 %collective-permute-start.40 = (f32[3,16384]{1,0:T(4,128)}, f32[3,16384]{1,0:T(4,128)S(1)}, u32[]{:S(2)}, u32[]{:S(2)}) collective-permute-start(f32[3,16384]{1,0:T(4,128)} %fusion.357), channel_id=1, source_target_pairs={{0,31},{1,0},{2,1},{3,2},{4,3},{5,4},{6,5},{7,6},{8,7},{9,8},{10,9... | collective-permute-start | bytes 589832 | tf_op jit(solution)/shard_map/ppermute | solution.py:14
  245.5 13.6 %collective-permute-start.41 = (f32[3,16384]{1,0:T(4,128)}, f32[3,16384]{1,0:T(4,128)S(1)}, u32[]{:S(2)}, u32[]{:S(2)}) collective-permute-start(f32[3,16384]{1,0:T(4,128)} %fusion.346), channel_id=1, source_target_pairs={{0,30},{1,31},{2,0},{3,1},{4,2},{5,3},{6,4},{7,5},{8,6},{9,7},{10,... | collective-permute-start | bytes 589832 | tf_op jit(solution)/shard_map/ppermute | solution.py:14
  245.6 13.6 %collective-permute-start.42 = (f32[3,16384]{1,0:T(4,128)}, f32[3,16384]{1,0:T(4,128)S(1)}, u32[]{:S(2)}, u32[]{:S(2)}) collective-permute-start(f32[3,16384]{1,0:T(4,128)} %fusion.335), channel_id=1, source_target_pairs={{0,1},{1,2},{2,3},{3,4},{4,5},{5,6},{6,7},{7,8},{8,9},{9,10},{10,1... | collective-permute-start | bytes 589832 | tf_op jit(solution)/shard_map/ppermute | solution.py:14
  245.7 27.0 %collective-permute-start.43 = (f32[3,16384]{1,0:T(4,128)}, f32[3,16384]{1,0:T(4,128)}, u32[]{:S(2)}, u32[]{:S(2)}) collective-permute-start(f32[3,16384]{1,0:T(4,128)} %fusion.324), channel_id=1, source_target_pairs={{0,2},{1,3},{2,4},{3,5},{4,6},{5,7},{6,8},{7,9},{8,10},{9,11},{10,... | collective-permute-start | bytes 589832 | tf_op jit(solution)/shard_map/ppermute | solution.py:14
  248.6 37.5 %collective-permute-start.16 = (f32[3,16384]{1,0:T(4,128)}, f32[3,16384]{1,0:T(4,128)}, u32[]{:S(2)}, u32[]{:S(2)}) collective-permute-start(f32[3,16384]{1,0:T(4,128)} %fusion.363), channel_id=1, source_target_pairs={{0,31},{1,0},{2,1},{3,2},{4,3},{5,4},{6,5},{7,6},{8,7},{9,8},{10,9... | collective-permute-start | bytes 589832 | tf_op jit(solution)/shard_map/ppermute | solution.py:14
  255.8 16.9 %copy-start.37 = (f32[3,16384]{1,0:T(4,128)}, f32[3,16384]{1,0:T(4,128)S(1)}, u32[]{:S(2)}) copy-start(f32[3,16384]{1,0:T(4,128)S(1)} %collective-permute-done.40) | copy-start | bytes 589828
  255.8 30.3 %collective-permute-start.17 = (f32[3,16384]{1,0:T(4,128)}, f32[3,16384]{1,0:T(4,128)}, u32[]{:S(2)}, u32[]{:S(2)}) collective-permute-start(f32[3,16384]{1,0:T(4,128)} %fusion.352), channel_id=1, source_target_pairs={{0,30},{1,31},{2,0},{3,1},{4,2},{5,3},{6,4},{7,5},{8,6},{9,7},{10,... | collective-permute-start | bytes 589832 | tf_op jit(solution)/shard_map/ppermute | solution.py:14
  259.1 13.6 %copy-start.40 = (f32[3,16384]{1,0:T(4,128)}, f32[3,16384]{1,0:T(4,128)S(1)}, u32[]{:S(2)}) copy-start(f32[3,16384]{1,0:T(4,128)S(1)} %collective-permute-done.41) | copy-start | bytes 589828
  259.1 26.9 %collective-permute-start.18 = (f32[3,16384]{1,0:T(4,128)}, f32[3,16384]{1,0:T(4,128)}, u32[]{:S(2)}, u32[]{:S(2)}) collective-permute-start(f32[3,16384]{1,0:T(4,128)} %fusion.341), channel_id=1, source_target_pairs={{0,1},{1,2},{2,3},{3,4},{4,5},{5,6},{6,7},{7,8},{8,9},{9,10},{10,1... | collective-permute-start | bytes 589832 | tf_op jit(solution)/shard_map/ppermute | solution.py:14
  259.1 13.6 %copy-start.43 = (f32[3,16384]{1,0:T(4,128)}, f32[3,16384]{1,0:T(4,128)S(1)}, u32[]{:S(2)}) copy-start(f32[3,16384]{1,0:T(4,128)S(1)} %collective-permute-done.42) | copy-start | bytes 589828
  259.1 26.9 %collective-permute-start.19 = (f32[3,16384]{1,0:T(4,128)}, f32[3,16384]{1,0:T(4,128)}, u32[]{:S(2)}, u32[]{:S(2)}) collective-permute-start(f32[3,16384]{1,0:T(4,128)} %fusion.330), channel_id=1, source_target_pairs={{0,2},{1,3},{2,4},{3,5},{4,6},{5,7},{6,8},{7,9},{8,10},{9,11},{10,... | collective-permute-start | bytes 589832 | tf_op jit(solution)/shard_map/ppermute | solution.py:14
  305.4 9.2 %collective-permute-start.20 = (f32[3,16384]{1,0:T(4,128)}, f32[3,16384]{1,0:T(4,128)S(1)}, u32[]{:S(2)}, u32[]{:S(2)}) collective-permute-start(f32[3,16384]{1,0:T(4,128)} %fusion.362), channel_id=1, source_target_pairs={{0,31},{1,0},{2,1},{3,2},{4,3},{5,4},{6,5},{7,6},{8,7},{9,8},{10,9... | collective-permute-start | bytes 589832 | tf_op jit(solution)/shard_map/ppermute | solution.py:14
  308.1 12.3 %collective-permute-start.21 = (f32[3,16384]{1,0:T(4,128)}, f32[3,16384]{1,0:T(4,128)S(1)}, u32[]{:S(2)}, u32[]{:S(2)}) collective-permute-start(f32[3,16384]{1,0:T(4,128)} %fusion.351), channel_id=1, source_target_pairs={{0,30},{1,31},{2,0},{3,1},{4,2},{5,3},{6,4},{7,5},{8,6},{9,7},{10,... | collective-permute-start | bytes 589832 | tf_op jit(solution)/shard_map/ppermute | solution.py:14
  308.1 12.3 %collective-permute-start.22 = (f32[3,16384]{1,0:T(4,128)}, f32[3,16384]{1,0:T(4,128)S(1)}, u32[]{:S(2)}, u32[]{:S(2)}) collective-permute-start(f32[3,16384]{1,0:T(4,128)} %fusion.340), channel_id=1, source_target_pairs={{0,1},{1,2},{2,3},{3,4},{4,5},{5,6},{6,7},{7,8},{8,9},{9,10},{10,1... | collective-permute-start | bytes 589832 | tf_op jit(solution)/shard_map/ppermute | solution.py:14
  308.3 13.5 %collective-permute-start.23 = (f32[3,16384]{1,0:T(4,128)}, f32[3,16384]{1,0:T(4,128)}, u32[]{:S(2)}, u32[]{:S(2)}) collective-permute-start(f32[3,16384]{1,0:T(4,128)} %fusion.329), channel_id=1, source_target_pairs={{0,2},{1,3},{2,4},{3,5},{4,6},{5,7},{6,8},{7,9},{8,10},{9,11},{10,... | collective-permute-start | bytes 589832 | tf_op jit(solution)/shard_map/ppermute | solution.py:14
  356.1 2.5 collective-permute-start.44
  361.8 6.2 %collective-permute-start.45 = (f32[128,13,13]{0,2,1:T(8,128)S(1)}, f32[128,13,13]{0,2,1:T(8,128)S(1)}, u32[]{:S(2)}, u32[]{:S(2)}) collective-permute-start(f32[128,13,13]{0,2,1:T(8,128)S(1)} %copy.122), channel_id=1, source_target_pairs={{0,2},{1,3},{2,0},{3,1},{4,6},{5,7},{6,4},{7,5},{8,10},{9,11},{10,... | collective-permute-start | bytes 259592 | tf_op jit(solution)/shard_map/ppermute | solution.py:101
  371.1 6.7 %collective-permute-start.46 = (f32[128,13,13]{0,2,1:T(8,128)S(1)}, f32[128,13,13]{0,2,1:T(8,128)S(1)}, u32[]{:S(2)}, u32[]{:S(2)}) collective-permute-start(f32[128,13,13]{0,2,1:T(8,128)S(1)} %copy.124), channel_id=1, source_target_pairs={{0,4},{1,5},{2,6},{3,7},{4,0},{5,1},{6,2},{7,3},{8,12},{9,13},{10,... | collective-permute-start | bytes 259592 | tf_op jit(solution)/shard_map/ppermute | solution.py:101
  380.9 4.7 %collective-permute-start.47 = (f32[128,13,13]{0,2,1:T(8,128)S(1)}, f32[128,13,13]{0,2,1:T(8,128)S(1)}, u32[]{:S(2)}, u32[]{:S(2)}) collective-permute-start(f32[128,13,13]{0,2,1:T(8,128)S(1)} %copy.126), channel_id=1, source_target_pairs={{0,8},{1,9},{2,10},{3,11},{4,12},{5,13},{6,14},{7,15},{8,0},{9,1},... | collective-permute-start | bytes 259592 | tf_op jit(solution)/shard_map/ppermute | solution.py:101
  388.8 6.2 %collective-permute-start.48 = (f32[128,13,13]{0,2,1:T(8,128)S(1)}, f32[128,13,13]{0,2,1:T(8,128)S(1)}, u32[]{:S(2)}, u32[]{:S(2)}) collective-permute-start(f32[128,13,13]{0,2,1:T(8,128)S(1)} %copy.128), channel_id=1, source_target_pairs={{0,16},{1,17},{2,18},{3,19},{4,20},{5,21},{6,22},{7,23},{8,24},{9,... | collective-permute-start | bytes 259592 | tf_op jit(solution)/shard_map/ppermute | solution.py:101
  (38 other events, 101.0 us)
